TPU v7x, 32 devices: a whole 2x2x4 slice. The times are simulated.
32 devices in a mesh: dp: 4 (over y, x), tensor: 8 (over z, core).
Axes of the slice: x: 2, y: 2, z: 4, core: 2. Of those that a mesh axis runs over, the one named last changes fastest.
Arguments:
- noisy: bfloat16 [32, 256, 1152], P('dp', None, 'tensor'), may hold values from -6 to 6
- labels: int32 [32], P('dp'), may hold values from 0 to 999
- tsteps: int32 [32], P('dp'), may hold values from 0 to 999
- guide_index: int32 [32], P('dp'), may hold values from 0 to 31
- class_table: bfloat16 [1001, 1152], replicated, may hold values from -6 to 6
- time_table: bfloat16 [1000, 1152], replicated, may hold values from -6 to 6
- guide_table: bfloat16 [32, 1152], replicated, may hold values from -6 to 6
- guide_weights: float32 [32], replicated, may hold values from 0.5 to 4
- teacher_qkv: bfloat16 [1152, 3456], P(None, 'tensor'), may hold values from -0.1875 to 0.1875
- teacher_out: bfloat16 [1152, 1152], P('tensor'), may hold values from -0.1875 to 0.1875
- teacher_ada: bfloat16 [3, 1152, 1152], P(None, None, 'tensor'), may hold values from -0.1875 to 0.1875
- student_qkv: bfloat16 [1152, 3456], P(None, 'tensor'), may hold values from -0.1875 to 0.1875
- student_out: bfloat16 [1152, 1152], P('tensor'), may hold values from -0.1875 to 0.1875
- student_ada: bfloat16 [3, 1152, 1152], P(None, None, 'tensor'), may hold values from -0.1875 to 0.1875
Outputs:
- grad_qkv: float32 [1152, 3456], P('dp', 'tensor')
- grad_out: float32 [1152, 1152], P('tensor', 'dp')
- grad_ada: float32 [3, 1152, 1152], P(None, 'dp', 'tensor')
All inputs are finite; a program needn't handle non-finite values.
Results may differ from a plain program's by a relative error of at most 0.034.
Values may be sent and summed in bfloat16 or wider, within the bound.
A program may use at most 128 MiB of HBM per device.

v0:
```python
import functools
import math

import jax
import jax.numpy as jnp
from jax import lax
from jax.experimental import pallas as pl
from jax.experimental.pallas import tpu as pltpu
from jax.sharding import PartitionSpec as P

HD = 72


norm_eps = 1e-06


def lookup_rows(indices, table_rows):
    one_hot = (
        indices[:, None] == jnp.arange(table_rows.shape[0], dtype=jnp.int32)[None, :]
    ).astype(table_rows.dtype)
    return jnp.dot(one_hot, table_rows, preferred_element_type=jnp.float32)


def attend(qkv_sums, heads_here):
    batch_rows, seq_len = (qkv_sums.shape[0], qkv_sums.shape[1])
    heads_qkv = qkv_sums.astype(jnp.bfloat16).reshape(batch_rows, seq_len, heads_here, 3, HD)
    queries, key_rows, values = (
        heads_qkv[:, :, :, 0],
        heads_qkv[:, :, :, 1],
        heads_qkv[:, :, :, 2],
    )
    scores = jnp.einsum(
        "blhe,bmhe->bhlm", queries, key_rows, preferred_element_type=jnp.float32
    ) * (1.0 / math.sqrt(HD))
    exponent = jnp.exp(scores - jnp.max(scores, axis=-1, keepdims=True))
    attn_prob = exponent / jnp.sum(exponent, axis=-1, keepdims=True)
    prob_low = attn_prob.astype(jnp.bfloat16)
    attn_mixed = jnp.einsum("bhlm,bmhe->bhel", prob_low, values, preferred_element_type=jnp.float32)
    attn_mixed = attn_mixed.astype(jnp.bfloat16).reshape(batch_rows, heads_here * HD, seq_len)
    return (heads_qkv, attn_prob, prob_low, attn_mixed)


def attend_grad(heads_qkv, attn_prob, prob_low, grad_low):
    batch_rows, seq_len = (heads_qkv.shape[0], heads_qkv.shape[1])
    queries, key_rows, values = (
        heads_qkv[:, :, :, 0],
        heads_qkv[:, :, :, 1],
        heads_qkv[:, :, :, 2],
    )
    grad_probs = jnp.einsum("bhel,bmhe->bhlm", grad_low, values, preferred_element_type=jnp.float32)
    row_delta = jnp.sum(attn_prob * grad_probs, axis=-1, keepdims=True)
    grad_scores = (attn_prob * (grad_probs - row_delta) * (1.0 / math.sqrt(HD))).astype(
        jnp.bfloat16
    )
    grad_query = jnp.einsum(
        "bhlm,bmhe->blhe", grad_scores, key_rows, preferred_element_type=jnp.float32
    )
    grad_keys = jnp.einsum(
        "bhlm,blhe->bmhe", grad_scores, queries, preferred_element_type=jnp.float32
    )
    grad_values = jnp.einsum(
        "bhlm,bhel->bmhe", prob_low, grad_low, preferred_element_type=jnp.float32
    )
    grad_qkv_act = jnp.stack([grad_query, grad_keys, grad_values], axis=3).astype(jnp.bfloat16)
    return grad_qkv_act.reshape(batch_rows, seq_len, -1)


def exchange_kernel(axis, slots, count, *refs):
    sources, landings = refs[:count], refs[count : 2 * count]
    send_sem, recv_sem, own_sem = refs[2 * count :]
    ways = lax.axis_size(axis)
    me = lax.axis_index(axis)
    barrier = pltpu.get_barrier_semaphore()
    for hop in range(1, ways):
        peer = lax.rem(me + hop, ways)
        pl.semaphore_signal(
            barrier, inc=1, device_id={axis: peer}, device_id_type=pl.DeviceIdType.MESH
        )
    pl.semaphore_wait(barrier, ways - 1)
    copies = []
    for hop in range(1, ways):
        peer = lax.rem(me + hop, ways)
        for item in range(count):
            take, put = slots[item]
            copy = pltpu.make_async_remote_copy(
                src_ref=take(sources[item], peer),
                dst_ref=put(landings[item], me),
                send_sem=send_sem.at[item, hop - 1],
                recv_sem=recv_sem.at[item, hop - 1],
                device_id={axis: peer},
                device_id_type=pl.DeviceIdType.MESH,
            )
            copy.start()
            copies.append(copy)
    for item in range(count):
        take, put = slots[item]
        copy = pltpu.make_async_copy(
            take(sources[item], me), put(landings[item], me), own_sem.at[item]
        )
        copy.start()
        copies.append(copy)
    for copy in copies:
        copy.wait()


def exchange(axis, collective, arrays, shapes, slots):
    ways = lax.axis_size(axis)
    count = len(arrays)
    return pl.pallas_call(
        functools.partial(exchange_kernel, axis, slots, count),
        out_shape=[jax.ShapeDtypeStruct(s, a.dtype) for s, a in zip(shapes, arrays)],
        in_specs=[pl.BlockSpec(memory_space=pltpu.VMEM)] * count,
        out_specs=[pl.BlockSpec(memory_space=pltpu.VMEM)] * count,
        scratch_shapes=[
            pltpu.SemaphoreType.DMA((count, ways - 1)),
            pltpu.SemaphoreType.DMA((count, ways - 1)),
            pltpu.SemaphoreType.DMA((count,)),
        ],
        compiler_params=pltpu.CompilerParams(collective_id=collective, has_side_effects=True),
        cost_estimate=pl.CostEstimate(flops=0, bytes_accessed=40000000, transcendentals=0),
    )(*arrays)


def block_of(ref, index):
    return ref.at[index]


def whole_of(ref, index):
    return ref


def modulate(normed, scale, shift):
    return (normed.astype(jnp.float32) * (1.0 + scale[:, None]) + shift[:, None]).astype(
        jnp.bfloat16
    )


def project_qkv(full_rows, qkv_weight):
    return jnp.einsum("bld,df->blf", full_rows, qkv_weight, preferred_element_type=jnp.float32)


def weight_grad_kernel(act_ref, grad_ref, scale_ref, shift_ref, weight_ref, out_ref, mod_ref, sum_ref):
    @pl.when(pl.program_id(0) == 0)
    def _():
        sum_ref[...] = jnp.zeros_like(sum_ref)

    grads = grad_ref[0]
    over_tokens = lax.dot_general(
        grads,
        jnp.ones((grads.shape[0], 128), jnp.bfloat16),
        (((0,), (0,)), ((), ())),
        preferred_element_type=jnp.float32,
    )[:, :1]
    width = act_ref.shape[2]
    step = 384 if width % 384 == 0 else 128
    for start in range(0, width, step):
        cols = pl.ds(start, step)
        product = lax.dot_general(
            grads, act_ref[0, :, cols], (((0,), (0,)), ((), ())), preferred_element_type=jnp.float32
        )
        weight = weight_ref[:, cols].astype(jnp.float32)
        mod_ref[0, 0:1, cols] = jnp.sum(weight * over_tokens, axis=0, keepdims=True)
        mod_ref[0, 1:2, cols] = jnp.sum(weight * product, axis=0, keepdims=True)
        sum_ref[:, cols] += product * (1.0 + scale_ref[0, :, cols]) + over_tokens * shift_ref[
            0, :, cols
        ]

    @pl.when(pl.program_id(0) == pl.num_programs(0) - 1)
    def _():
        for start in range(0, width, step):
            cols = pl.ds(start, step)
            out_ref[cols, :] = sum_ref[:, cols].T.astype(out_ref.dtype)


def weight_grad(normed, grad_qkv_act, scale, shift, weight_t):
    samples, seq_len, width = normed.shape
    columns = grad_qkv_act.shape[2]
    return pl.pallas_call(
        weight_grad_kernel,
        grid=(samples,),
        in_specs=[
            pl.BlockSpec((1, seq_len, width), lambda b: (b, 0, 0)),
            pl.BlockSpec((1, seq_len, columns), lambda b: (b, 0, 0)),
            pl.BlockSpec((1, 1, width), lambda b: (b, 0, 0)),
            pl.BlockSpec((1, 1, width), lambda b: (b, 0, 0)),
            pl.BlockSpec((columns, width), lambda b: (0, 0)),
        ],
        out_specs=[
            pl.BlockSpec((width, columns), lambda b: (0, 0)),
            pl.BlockSpec((1, 2, width), lambda b: (b, 0, 0)),
        ],
        out_shape=[
            jax.ShapeDtypeStruct((width, columns), jnp.bfloat16),
            jax.ShapeDtypeStruct((samples, 2, width), jnp.float32),
        ],
        scratch_shapes=[pltpu.VMEM((columns, width), jnp.float32)],
        compiler_params=pltpu.CompilerParams(
            dimension_semantics=("arbitrary",), vmem_limit_bytes=32 * 1024 * 1024
        ),
        cost_estimate=pl.CostEstimate(
            flops=2 * samples * seq_len * width * columns,
            bytes_accessed=samples * seq_len * (width + columns) * 2 + width * columns * 6,
            transcendentals=0,
        ),
    )(normed, grad_qkv_act, scale[:, None], shift[:, None], weight_t)


def local(
    noisy,
    labels,
    tsteps,
    guide_index,
    class_table,
    time_table,
    guide_table,
    guide_weights,
    teacher_qkv,
    teacher_out,
    teacher_ada,
    student_qkv,
    student_out,
    student_ada,
):
    samples, seq_len, width_part = noisy.shape
    ways = lax.axis_size("tensor")
    groups = lax.axis_size("dp")
    me = lax.axis_index("tensor")
    model_width = width_part * ways
    batch_size = samples * groups
    wide_noisy = lax.all_gather(noisy, "tensor", axis=2, tiled=True)

    null_class = class_table.shape[0] - 1
    time_embed = lookup_rows(tsteps, time_table)
    cond_embed = lookup_rows(labels, class_table) + time_embed
    null_embed = class_table[null_class].astype(jnp.float32)[None, :] + time_embed
    guide_hot = guide_index[:, None] == jnp.arange(guide_table.shape[0], dtype=jnp.int32)[None, :]
    student_embed = cond_embed + jnp.dot(
        guide_hot.astype(jnp.bfloat16), guide_table, preferred_element_type=jnp.float32
    )
    strength = jnp.sum(jnp.where(guide_hot, guide_weights[None, :], 0.0), axis=1)
    cond_act = jax.nn.silu(cond_embed).astype(jnp.bfloat16)
    null_act = jax.nn.silu(null_embed).astype(jnp.bfloat16)
    student_act = jax.nn.silu(student_embed).astype(jnp.bfloat16)
    teacher_act = jnp.concatenate([cond_act, null_act], axis=0)
    mod_teacher = jnp.einsum(
        "bd,kde->kbe", teacher_act, teacher_ada, preferred_element_type=jnp.float32
    )
    mod_student = jnp.einsum(
        "bd,kde->kbe", student_act, student_ada, preferred_element_type=jnp.float32
    )
    mods = jnp.concatenate([mod_student, mod_teacher], axis=1).reshape(-1, width_part)
    wide_mods = gather_mods(mods).reshape(3, 3, samples, model_width)
    shift, scale, gate = wide_mods[0], wide_mods[1], wide_mods[2]

    teacher_out_full = lax.all_gather(teacher_out, "tensor", axis=0, tiled=True)
    student_out_full = lax.all_gather(student_out, "tensor", axis=0, tiled=True)

    signal = wide_noisy.astype(jnp.float32)
    row_mean = jnp.sum(signal, axis=2, keepdims=True) / model_width
    row_var = jnp.sum(signal * signal, axis=2, keepdims=True) / model_width - row_mean * row_mean
    normed = ((signal - row_mean) * lax.rsqrt(row_var + norm_eps)).astype(jnp.bfloat16)
    normed = lax.optimization_barrier(normed)

    heads_here = student_out.shape[0] // HD
    teacher_rows = jnp.concatenate(
        [modulate(normed, scale[1], shift[1]), modulate(normed, scale[2], shift[2])], axis=0
    )
    unused_qkv, unused_prob, unused_low, teacher_mixed = attend(
        project_qkv(teacher_rows, teacher_qkv), heads_here
    )
    student_rows = modulate(normed, scale[0], shift[0])
    heads_qkv, attn_prob, prob_low, student_mixed = attend(
        project_qkv(student_rows, student_qkv), heads_here
    )
    head_cols = heads_here * HD
    row_count = samples * seq_len // ways
    run = min(row_count, seq_len)
    images = row_count // run

    def rows_of(device):
        start = lax.rem(device * row_count, seq_len) if run < seq_len else 0
        if run < seq_len and run % 128 == 0:
            start = pl.multiple_of(start, 128)
        return pl.ds(device * row_count // seq_len, images), pl.ds(start, run)

    def take_tokens(ref, device):
        which, rows = rows_of(device)
        return ref.at[:, which, :, rows] if run < seq_len else ref.at[:, which]

    mixed = jnp.concatenate([student_mixed, teacher_mixed], axis=0).reshape(
        3, samples, head_cols, seq_len
    )
    (mixed_rows,) = exchange(
        "tensor",
        0,
        [mixed],
        [(ways, 3, images, head_cols, run)],
        [(take_tokens, block_of)],
    )
    first = me * row_count // seq_len
    own_gate = lax.dynamic_slice_in_dim(gate, first, images, axis=1)
    own_strength = lax.dynamic_slice_in_dim(strength, first, images, axis=0)[:, None]
    mixed_rows = mixed_rows.transpose(1, 2, 0, 3, 4).reshape(3, images, model_width, run)
    student_proj = jnp.einsum(
        "ier,ed->ird", mixed_rows[0], student_out_full, preferred_element_type=jnp.float32
    )
    teacher_proj = jnp.einsum(
        "kier,ed->kird", mixed_rows[1:], teacher_out_full, preferred_element_type=jnp.float32
    )
    scale_norm = 1.0 / math.sqrt(batch_size * seq_len)
    cotangent = scale_norm * (
        own_gate[0][:, None] * student_proj
        - ((1.0 + own_strength) * own_gate[1])[:, None] * teacher_proj[0]
        + (own_strength * own_gate[2])[:, None] * teacher_proj[1]
    )
    own_grad_gate = jnp.sum(cotangent * student_proj, axis=1)
    grad_proj = (cotangent * own_gate[0][:, None]).astype(jnp.bfloat16)
    grad_mixed_rows = (
        jnp.einsum("ed,ird->eir", student_out_full, grad_proj, preferred_element_type=jnp.float32)
        .astype(jnp.bfloat16)
        .reshape(ways, head_cols, images, run)
        .transpose(0, 2, 1, 3)
    )

    def put_heads(ref, device):
        which, rows = rows_of(device)
        return ref.at[which, :, rows] if run < seq_len else ref.at[which]

    (grad_low,) = exchange(
        "tensor",
        1,
        [grad_mixed_rows],
        [(samples, head_cols, seq_len)],
        [(block_of, put_heads)],
    )
    grad_low = grad_low.reshape(samples, heads_here, HD, seq_len)
    late_proj, grad_low = lax.optimization_barrier((grad_proj, grad_low))
    grad_out_part = jnp.einsum(
        "ier,ird->ed", mixed_rows[0], late_proj, preferred_element_type=jnp.float32
    ).astype(jnp.bfloat16)
    grad_out_rows = lax.psum_scatter(grad_out_part, "tensor", scatter_dimension=0, tiled=True)

    grad_qkv_act = attend_grad(heads_qkv, attn_prob, prob_low, grad_low)
    grad_qkv_part, grad_mod = weight_grad(
        normed, grad_qkv_act, scale[0], shift[0], student_qkv.T
    )
    grad_gate = lax.dynamic_update_slice_in_dim(
        jnp.zeros((samples, model_width), jnp.float32), own_grad_gate, first, axis=0
    )
    grad_mod = jnp.concatenate([grad_mod, grad_gate[:, None]], axis=1).reshape(
        samples * 3, ways, width_part
    )
    (mod_terms,) = exchange(
        "tensor",
        2,
        [grad_mod.transpose(1, 0, 2)],
        [(ways, samples * 3, width_part)],
        [(block_of, block_of)],
    )
    own_mod = jnp.sum(mod_terms, axis=0)
    depth = model_width // groups
    qkv_terms, out_terms, wide_grad, act_all = exchange(
        "dp",
        3,
        [
            grad_qkv_part.reshape(groups, depth, head_cols * 3),
            grad_out_rows.reshape(head_cols, groups, depth).transpose(1, 0, 2),
            own_mod,
            student_act,
        ],
        [
            (groups, depth, head_cols * 3),
            (groups, head_cols, depth),
            (groups, samples * 3, width_part),
            (groups, samples, model_width),
        ],
        [(block_of, block_of), (block_of, block_of), (whole_of, block_of), (whole_of, block_of)],
    )
    grad_qkv = jnp.sum(qkv_terms.astype(jnp.float32), axis=0)
    grad_out = jnp.sum(out_terms.astype(jnp.float32), axis=0)
    own_act = lax.dynamic_slice_in_dim(act_all, lax.axis_index("dp") * depth, depth, axis=2)
    grad_ada = jnp.einsum(
        "bd,bke->kde",
        own_act.reshape(batch_size, depth).astype(jnp.float32),
        wide_grad.reshape(batch_size, 3, width_part),
        precision=lax.Precision.HIGHEST,
    )
    return (grad_qkv, grad_out, grad_ada)


def gather_mods(mods):
    gathered = lax.all_gather(mods, "tensor", axis=0)
    return gathered.transpose(1, 0, 2)


def solution(mesh):
    return jax.shard_map(
        local,
        mesh=mesh,
        in_specs=(
            P("dp", None, "tensor"),
            P("dp"),
            P("dp"),
            P("dp"),
            P(),
            P(),
            P(),
            P(),
            P(None, "tensor"),
            P("tensor", None),
            P(None, None, "tensor"),
            P(None, "tensor"),
            P("tensor", None),
            P(None, None, "tensor"),
        ),
        out_specs=(P("dp", "tensor"), P("tensor", "dp"), P(None, "dp", "tensor")),
        check_vma=False,
    )
```

profile of v0, /device:TPU:0, one launch (start us, length us, event | category | flops | bytes accessed | tf_op | source)
XLA Modules:
  0.0 299.5 jit_solution(14737493195651390234)
XLA Ops:
  16.3 20.1 %all_gather.13 = f32[8,72,144]{2,1,0:T(8,128)S(1)} all-gather(f32[1,72,144]{2,1,0:T(8,128)S(1)} %bitcast.154), channel_id=1, replica_groups=mesh['dp'=4,'tensor'=8] {'tensor'}, dimensions={0}, use_global_device_ids=true | all-gather | bytes 373248 | tf_op jit(solution)/shard_map/all_gather | solution.py:392
  39.6 27.9 %all-gather.4.cloned.1.call-done = bf16[8,256,1152]{1,0,2:T(8,128)(2,1)} async-done(((bf16[8,256,144]{1,0,2:T(8,128)(2,1)}), bf16[8,256,1152]{1,0,2:T(8,128)(2,1)}) %all-gather.4.cloned.1.call-update) | async-done | bytes 4718608 | tf_op jit(solution)/shard_map/all_gather | solution.py:230
  67.5 7.0 %copy.108 = bf16[8,256,1152]{2,1,0:T(8,128)(2,1)} copy(bf16[8,256,1152]{1,0,2:T(8,128)(2,1)} %all-gather.4.cloned.1.call-done) | data formatting | bytes 9437184 | tf_op jit(solution)/shard_map/all_gather | solution.py:230
  74.6 4.1 %convert_reduce_fusion = (f32[8,256]{1,0:T(8,128)S(1)}, f32[8,256]{1,0:T(8,128)S(1)}) fusion(bf16[8,256,1152]{2,1,0:T(8,128)(2,1)} %copy.108), kind=kLoop, calls=%fused_computation.8 | loop fusion | flops 9433088 | bytes 4734976 | tf_op jit(solution)/shard_map/reduce_sum | solution.py:259
  80.0 2.6 fusion.46
  83.4 4.5 %fusion.9 = (bf16[8,256,1152]{2,1,0:T(8,128)(2,1)S(1)}, bf16[8,256,1152]{2,1,0:T(8,128)(2,1)}) fusion(bf16[8,256,1152]{2,1,0:T(8,128)(2,1)S(1)} %fusion.4.act_ref, f32[8,1152]{1,0:T(8,128)S(1)} %add.141, f32[8,1152]{1,0:T(8,128)S(1)} %add.140, f32[8,1152]{1,0:T(8,128)S(1)} %add.146, f32[8,1152]{1,0:T(8,128)S(1)} %add.145), kind=kLoop, calls=%fused_computation.15 | loop fusion | flops 16515072 | bytes 14303232 | tf_op jit(solution)/shard_map/convert_element_type | solution.py:133
  87.9 3.2 %fusion.100 = (f32[8,2,256]{2,1,0:T(2,128)S(1)}, f32[8,2,256,256]{2,3,1,0:T(8,128)}) fusion(f32[8,2,256,256]{2,3,1,0:T(8,128)S(1)} %fusion.73), kind=kOutput, calls=%fused_computation.136 | output fusion | flops 4194559 | bytes 8404992 | tf_op jit(solution)/shard_map/sub | solution.py:35
  92.1 6.6 %fusion.40 = bf16[16,256,432]{1,2,0:T(8,128)(2,1)} fusion(bf16[8,256,1152]{2,1,0:T(8,128)(2,1)S(1)} %copy-done.7, bf16[8,256,1152]{2,1,0:T(8,128)(2,1)S(1)} %get-tuple-element.26, bf16[1152,432]{0,1:T(8,128)(2,1)S(1)} %copy-done.16), kind=kOutput, calls=%fused_computation.44 | convolution fusion | flops 4083351552 | bytes 13971456 | tf_op jit(solution)/shard_map/bld,df->blf/dot_general | solution.py:139
  98.6 3.1 %fusion.67 = f32[16,2,256,256]{2,3,1,0:T(8,128)S(1)} fusion(bf16[16,256,2,3,72]{1,4,3,2,0:T(8,128)(2,1)} %bitcast.149), kind=kOutput, calls=%fused_computation.71 | convolution fusion | flops 301989888 | bytes 10747904 | tf_op jit(solution)/shard_map/blhe,bmhe->bhlm/dot_general | solution.py:32
  102.3 6.3 %fusion.99 = (f32[16,2,256]{2,1,0:T(2,128)S(1)}, f32[16,2,256,256]{2,3,1,0:T(8,128)S(1)}) fusion(f32[16,2,256,256]{2,3,1,0:T(8,128)S(1)} %fusion.67), kind=kOutput, calls=%fused_computation.135 | output fusion | flops 8388863 | bytes 16809984 | tf_op jit(solution)/shard_map/sub | solution.py:35
  112.2 50.6 %shard_map.157 = bf16[8,3,1,144,256]{4,3,2,1,0:T(8,128)(2,1)} custom-call(bf16[3,8,144,256]{3,2,1,0:T(8,128)(2,1)} %bitcast.131), custom_call_target="tpu_custom_call" | custom-call | bytes 40000000 | tf_op jit(solution)/shard_map/pallas_call | solution.py:109
  165.4 5.1 %fusion.31 = f32[2,256,1152]{2,1,0:T(8,128)} fusion(bf16[2,1152,256]{2,1,0:T(8,128)(2,1)S(1)} %bitcast.135, bf16[1152,1152]{1,0:T(8,128)(2,1)} %all-gather.8.cloned.1.call-done), kind=kOutput, calls=%fused_computation.38 | convolution fusion | flops 1358954496 | bytes 6193152 | tf_op jit(solution)/shard_map/kier,ed->kird/dot_general | solution.py:307
  170.5 3.8 %multiply_reduce_fusion.3 = (f32[1152]{0:T(1024)S(1)}, f32[256,1152]{1,0:T(8,128)S(1)}) fusion(f32[2,256,1152]{2,1,0:T(8,128)} %fusion.31, f32[1152]{0:T(1024)S(1)} %get-tuple-element.23, f32[1152]{0:T(1024)S(1)} %get-tuple-element.22, f32[1152]{0:T(1024)S(1)} %get-tuple-element.21, bf16[1152,256]{1,0:T(8,128)(2,1)S(1)} %bitcast.136, ...), kind=kOutput, calls=%fused_computation.74 | convolution fusion | flops 681835392 | bytes 6801408 | tf_op jit(solution)/shard_map/ier,ed->ird/dot_general | solution.py:304
  176.5 25.7 %shard_map.158 = bf16[8,144,256]{2,1,0:T(8,128)(2,1)} custom-call(bf16[8,1,144,256]{3,2,1,0:T(8,128)(2,1)} %bitcast.140), custom_call_target="tpu_custom_call" | custom-call | bytes 40000000 | tf_op jit(solution)/shard_map/pallas_call | solution.py:109
  202.2 2.4 convolution_convert_fusion
  205.0 3.8 %fusion.74 = f32[8,2,256,256]{2,3,1,0:T(8,128)} fusion(bf16[8,2,72,256]{3,2,1,0:T(8,128)(2,1)S(1)} %bitcast.141, bf16[8,256,2,3,72]{1,4,3,2,0:T(8,128)(2,1)} %bitcast.146), kind=kOutput, calls=%fused_computation.88 | convolution fusion | flops 150994944 | bytes 5373952 | tf_op jit(solution)/shard_map/bhel,bmhe->bhlm/dot_general | solution.py:50
  208.8 7.6 %fusion.60 = bf16[8,256,2,1,72]{1,4,2,0,3:T(8,128)(2,1)S(1)} fusion(f32[8,2,256,256]{2,3,1,0:T(8,128)} %fusion.74, bf16[8,256,2,3,72]{1,4,3,2,0:T(8,128)(2,1)} %bitcast.147, f32[8,2,256,256]{2,3,1,0:T(8,128)} %get-tuple-element.44, f32[8,2,256]{2,1,0:T(2,128)S(1)} %get-tuple-element.43), kind=kOutput, calls=%fused_computation.63 | convolution fusion | flops 158634240 | bytes 17989632 | tf_op jit(solution)/shard_map/bhlm,bmhe->blhe/dot_general | solution.py:55
  216.4 7.5 %fusion.57 = bf16[8,256,2,1,72]{1,4,2,0,3:T(8,128)(2,1)S(1)} fusion(f32[8,2,256,256]{2,3,1,0:T(8,128)} %fusion.74, bf16[8,256,2,3,72]{1,4,3,2,0:T(8,128)(2,1)} %bitcast.148, f32[8,2,256,256]{2,3,1,0:T(8,128)} %get-tuple-element.44, f32[8,2,256]{2,1,0:T(2,128)S(1)} %get-tuple-element.43), kind=kOutput, calls=%fused_computation.62 | convolution fusion | flops 158634240 | bytes 17989632 | tf_op jit(solution)/shard_map/bhlm,blhe->bmhe/dot_general | solution.py:58
  224.0 3.0 %fusion.56 = bf16[8,256,2,1,72]{1,4,2,0,3:T(8,128)(2,1)S(1)} fusion(bf16[8,2,72,256]{3,2,1,0:T(8,128)(2,1)S(1)} %bitcast.142, f32[8,2,256,256]{2,3,1,0:T(8,128)} %get-tuple-element.44, f32[8,2,256]{2,1,0:T(2,128)S(1)} %get-tuple-element.43), kind=kOutput, calls=%fused_computation.61 | convolution fusion | flops 153387008 | bytes 5390336 | tf_op jit(solution)/shard_map/bhlm,bhel->bmhe/dot_general | solution.py:61
  228.5 2.8 copy.133.grad_ref
  231.3 2.4 copy-done.3
  233.7 8.1 %shard_map.159 = (bf16[1152,432]{1,0:T(8,128)(2,1)S(1)}, f32[8,2,1152]{2,1,0:T(2,128)S(1)}) custom-call(bf16[8,256,1152]{2,1,0:T(8,128)(2,1)S(1)} %copy-done.3, bf16[8,256,432]{2,1,0:T(8,128)(2,1)S(1)} %copy.133.grad_ref, f32[8,1,1152]{2,1,0:T(1,128)S(1)} %broadcast_in_dim_squeeze.4.scale_ref, f32[8,1,1152]{2,1,0:T(1,128)S(1)} %broadcast_in_dim_squeeze.5.shift_ref, ...), custom_call_target="tpu_custom_call" | custom-call | flops 2038431744 | bytes 9474048 | tf_op jit(solution)/shard_map/pallas_call | solution.py:178
  243.9 11.9 %shard_map.160 = f32[8,24,144]{2,1,0:T(8,128)} custom-call(f32[8,24,144]{2,1,0:T(8,128)} %bitcast.152), custom_call_target="tpu_custom_call" | custom-call | bytes 40000000 | tf_op jit(solution)/shard_map/pallas_call | solution.py:109
  259.5 26.3 %shard_map.161 = (bf16[4,288,432]{2,1,0:T(8,128)(2,1)}, bf16[4,144,288]{2,1,0:T(8,128)(2,1)}, f32[4,24,144]{2,1,0:T(8,128)}, bf16[4,8,1152]{2,1,0:T(8,128)(2,1)}) custom-call(bf16[4,288,432]{2,1,0:T(8,128)(2,1)} %bitcast.129, bf16[4,144,288]{2,1,0:T(8,128)(2,1)} %bitcast.143, f32[24,144]{1,0:T(8,128)} %reduce_sum.97.refs_2_, bf16[8,1152]{1,0:T(8,128)(2,1)} %copy-done.13), custom_call_target="tpu_custom_call" | custom-call | bytes 40000000 | tf_op jit(solution)/shard_map/pallas_call | solution.py:109
  (107 shorter events, 38.1 us)
Async XLA Ops:
  7.2 4.7 %copy-start = (bf16[1000,1152]{1,0:T(8,128)(2,1)S(1)}, bf16[1000,1152]{1,0:T(8,128)(2,1)}, u32[]{:S(2)}) copy-start(bf16[1000,1152]{1,0:T(8,128)(2,1)} %param.19) | copy-start | bytes 6912004
  7.2 5.8 %copy-start.14 = (s32[8]{0:T(128)S(1)}, s32[8]{0:T(128)}, u32[]{:S(2)}) copy-start(s32[8]{0:T(128)} %param.15) | copy-start | bytes 100
  7.2 8.0 %copy-start.18 = (s32[8]{0:T(128)S(1)}, s32[8]{0:T(128)}, u32[]{:S(2)}) copy-start(s32[8]{0:T(128)} %param.17) | copy-start | bytes 100
  7.2 8.0 %copy-start.17 = (bf16[32,1152]{1,0:T(8,128)(2,1)S(1)}, bf16[32,1152]{1,0:T(8,128)(2,1)}, u32[]{:S(2)}) copy-start(bf16[32,1152]{1,0:T(8,128)(2,1)} %param.20) | copy-start | bytes 221188
  7.2 8.7 %copy-start.11 = (bf16[3,1152,144]{1,2,0:T(8,128)(2,1)S(1)}, bf16[3,1152,144]{1,2,0:T(8,128)(2,1)}, u32[]{:S(2)}) copy-start(bf16[3,1152,144]{1,2,0:T(8,128)(2,1)} %param.24) | copy-start | bytes 2985988
  7.2 60.3 %all-gather.4.cloned.1.call-start = ((), (), s32[]{:S(2)}) async-start(), calls=%async_computation.1 | async-start | bytes 5308416 | tf_op jit(solution)/shard_map/all_gather | solution.py:230
  9.5 155.9 %all-gather.8.cloned.1.call-start = ((), (), s32[]{:S(2)}) async-start(), calls=%async_computation.3 | async-start | bytes 2985984 | tf_op jit(solution)/shard_map/all_gather | solution.py:255
  10.3 160.2 %all-gather.6.cloned.1.call-start = ((), (), s32[]{:S(2)}) async-start(), calls=%async_computation.2 | async-start | bytes 2985984 | tf_op jit(solution)/shard_map/all_gather | solution.py:256
  11.0 246.4 %reduce-scatter.2.cloned.1.call-start = ((), (), s32[]{:S(2)}) async-start(), calls=%async_computation.4 | async-start | bytes 2985984 | tf_op jit(solution)/shard_map/reduce_scatter | solution.py:341
  11.1 4.4 %copy-start.12 = (bf16[3,1152,144]{1,2,0:T(8,128)(2,1)S(1)}, bf16[3,1152,144]{1,2,0:T(8,128)(2,1)}, u32[]{:S(2)}) copy-start(bf16[3,1152,144]{1,2,0:T(8,128)(2,1)} %param.27) | copy-start | bytes 2985988
  13.0 24.2 %copy-start.19 = (f32[32]{0:T(128)S(1)}, f32[32]{0:T(128)}, u32[]{:S(2)}) copy-start(f32[32]{0:T(128)} %param.21) | copy-start | bytes 388
  15.4 59.1 %copy-start.13 = (bf16[8,1152]{1,0:T(8,128)(2,1)}, bf16[8,1152]{1,0:T(8,128)(2,1)S(1)}, u32[]{:S(2)}) copy-start(bf16[8,1152]{1,0:T(8,128)(2,1)S(1)} %multiply_convert_fusion.5.refs_3_) | copy-start | bytes 55300
  74.6 4.2 %copy-start.6 = (bf16[8,256,1152]{2,1,0:T(8,128)(2,1)S(1)}, bf16[8,256,1152]{2,1,0:T(8,128)(2,1)}, u32[]{:S(2)}) copy-start(bf16[8,256,1152]{2,1,0:T(8,128)(2,1)} %copy.108) | copy-start | bytes 14155780
  78.7 1.3 copy-start.5
  80.0 3.3 %copy-start.2 = (bf16[8,256,1152]{2,1,0:T(8,128)(2,1)}, bf16[8,256,1152]{2,1,0:T(8,128)(2,1)S(1)}, u32[]{:S(2)}) copy-start(bf16[8,256,1152]{2,1,0:T(8,128)(2,1)S(1)} %fusion.4.act_ref) | copy-start | bytes 14155780
  82.6 19.1 %copy-start.10 = (bf16[8,256,432]{1,2,0:T(8,128)(2,1)}, bf16[8,256,432]{1,2,0:T(8,128)(2,1)S(1)}, u32[]{:S(2)}) copy-start(bf16[8,256,432]{1,2,0:T(8,128)(2,1)S(1)} %fusion.46) | copy-start | bytes 5308420
  87.9 3.3 %copy-start.7 = (bf16[8,256,1152]{2,1,0:T(8,128)(2,1)S(1)}, bf16[8,256,1152]{2,1,0:T(8,128)(2,1)}, u32[]{:S(2)}) copy-start(bf16[8,256,1152]{2,1,0:T(8,128)(2,1)} %get-tuple-element.27) | copy-start | bytes 14155780
  87.9 4.2 %copy-start.16 = (bf16[1152,432]{0,1:T(8,128)(2,1)S(1)}, bf16[1152,432]{0,1:T(8,128)(2,1)}, u32[]{:S(2)}) copy-start(bf16[1152,432]{0,1:T(8,128)(2,1)} %param.22) | copy-start | bytes 2985988
  98.6 3.1 %copy-start.8 = (f32[8,2,256,256]{2,3,1,0:T(8,128)S(1)}, f32[8,2,256,256]{2,3,1,0:T(8,128)}, u32[]{:S(2)}) copy-start(f32[8,2,256,256]{2,3,1,0:T(8,128)} %get-tuple-element.44) | copy-start | bytes 12582916
  170.5 3.9 %copy-start.15 = (bf16[1152,1152]{1,0:T(8,128)(2,1)S(1)}, bf16[1152,1152]{1,0:T(8,128)(2,1)}, u32[]{:S(2)}) copy-start(bf16[1152,1152]{1,0:T(8,128)(2,1)} %all-gather.6.cloned.1.call-done) | copy-start | bytes 7962628
  202.2 2.7 copy-start.9
  231.3 2.4 copy-start.3
  241.8 1.0 copy-start.4
  242.9 50.1 %copy-start.1 = (bf16[1000,1152]{1,0:T(8,128)(2,1)S(1)}, bf16[1000,1152]{1,0:T(8,128)(2,1)}, u32[]{:S(2)}) copy-start(bf16[1000,1152]{1,0:T(8,128)(2,1)} %param.19) | copy-start | bytes 6912004
Sparse Core Ops, SparseCore 0:
  10.2 57.2 all-gather.3
  69.1 33.6 all-gather.7
  104.5 61.5 all-gather.5
  204.8 41.4 reduce-scatter.1
where the time goes:
time: 301 us; the launch traced here: 300 us
  Pallas kernels  123 us (41%)
  matrix products  56.5 us (19%)
  waiting for transfers between devices  29.4 us (10%)
  other arithmetic  28.6 us (10%)
  local copies, waits for them, and re-layouts  27.3 us (9%)
  blocking collectives  20.1 us (7%)
  between operations  15 us (5%)
    pallas_call x4, Pallas kernels, exchange(): pl.pallas_call(functools.partial(exchange_kernel, axis, slots, count), ou...  114 us
    all_gather x1, waiting for transfers between devices, local(): wide_noisy = lax.all_gather(noisy, 'tensor', axis=2, tiled=True)  27.9 us
    all_gather x1, blocking collectives, gather_mods(): gathered = lax.all_gather(mods, 'tensor', axis=0)  20.1 us
    sub x2, other arithmetic, attend(): exponent = jnp.exp(scores - jnp.max(scores, axis=-1, keepdims=True))  9.56 us
    dot_general x2, matrix products, project_qkv(): jnp.einsum('bld,df->blf', full_rows, qkv_weight, preferred_element_type=j...  9.12 us
    pallas_call x1, Pallas kernels, weight_grad(): pl.pallas_call(weight_grad_kernel, grid=(samples,), in_specs=[pl.BlockSpe...  8.08 us
    dot_general x1, matrix products, attend_grad(): jnp.einsum('bhlm,bmhe->blhe', grad_scores, key_rows, preferred_element_ty...  7.61 us
    dot_general x1, matrix products, attend_grad(): jnp.einsum('bhlm,blhe->bmhe', grad_scores, queries, preferred_element_typ...  7.52 us
  transfers between devices with their start and end apart: 4, of which 1 were waited for; matrix products, arithmetic and copies ran while one was open for 29% of the time, Pallas kernels for 24%

commit v1 on v0

v1 whole, which is shorter than its diff:
```python
import functools
import math

import jax
import jax.numpy as jnp
from jax import lax
from jax.experimental import pallas as pl
from jax.experimental.pallas import tpu as pltpu
from jax.sharding import PartitionSpec as P

HD = 72
MESH = pl.DeviceIdType.MESH
F32 = jnp.float32
BF16 = jnp.bfloat16

norm_eps = 1e-06
LOG2E = math.log2(math.e)


def lookup_rows(indices, table_rows):
    one_hot = (
        indices[:, None] == jnp.arange(table_rows.shape[0], dtype=jnp.int32)[None, :]
    ).astype(table_rows.dtype)
    return jnp.dot(one_hot, table_rows, preferred_element_type=F32)


def dot_nn(a, b):
    return lax.dot_general(a, b, (((1,), (0,)), ((), ())), preferred_element_type=F32)


def dot_tn(a, b):
    return lax.dot_general(a, b, (((0,), (0,)), ((), ())), preferred_element_type=F32)


def dot_nt(a, b):
    return lax.dot_general(a, b, (((1,), (1,)), ((), ())), preferred_element_type=F32)


def step_kernel(
    sizes,
    noisy,
    act_s,
    act_t,
    strength,
    ada_s,
    ada_t,
    wq_s,
    wq_t,
    wo_s,
    wo_t,
    out_qkv,
    out_go,
    out_mod,
    out_act,
    xt,
    mg,
    mr,
    rows_tmp,
    colbuf,
    nt,
    md,
    qs,
    et,
    rinv,
    ms,
    mx,
    psend,
    ppart,
    pleft,
    pright,
    psum,
    gp,
    gq,
    go,
    gm,
    mt_send,
    mt_land,
    gqt,
    qk_send,
    qk_land,
    go_send,
    go_land,
    ag_send,
    ag_recv,
    pt_send,
    pt_recv,
    up_send,
    left_recv,
    right_recv,
    gp_send,
    gp_recv,
    mt_ssem,
    mt_rsem,
    dp_ssem,
    dp_rsem,
    own_sem,
):
    B, L, D, n, groups, heads, scale_norm = sizes
    nz = n // 2
    wp = D // n
    hc = heads * HD
    depth = D // groups
    chunk = 384 if D % 384 == 0 else 128
    col_chunks = [pl.ds(start, chunk) for start in range(0, D, chunk)]
    me = lax.axis_index("tensor")
    me_dp = lax.axis_index("dp")
    z = lax.div(me, 2)
    c = lax.rem(me, 2)
    partner = 2 * z + (1 - c)
    right = lax.rem(me + 2, n)
    left = lax.rem(me + n - 2, n)
    has_left = z > 0
    has_right = z < nz - 1
    first_fwd = nz
    first_sum = nz + 1
    first_bwd = nz + 1 + 2 * (nz - 1)
    soft = LOG2E / math.sqrt(HD)

    def remote(src, dst, ssem, rsem, target):
        return pltpu.make_async_remote_copy(
            src_ref=src,
            dst_ref=dst,
            send_sem=ssem,
            recv_sem=rsem,
            device_id={"tensor": target},
            device_id_type=MESH,
        )

    def remote_dp(src, dst, ssem, rsem, target):
        return pltpu.make_async_remote_copy(
            src_ref=src,
            dst_ref=dst,
            send_sem=ssem,
            recv_sem=rsem,
            device_id={"dp": target},
            device_id_type=MESH,
        )

    def place(k):
        pair = lax.div(k, 4)
        item = k - 4 * pair
        zo = pair + lax.rem(item, 2) * (nz - 1 - 2 * pair)
        co = lax.div(item, 2)
        return zo, co, k

    barrier = pltpu.get_barrier_semaphore()
    for hop in range(1, n):
        pl.semaphore_signal(
            barrier, inc=1, device_id={"tensor": lax.rem(me + hop, n)}, device_id_type=MESH
        )
    for hop in range(1, groups):
        pl.semaphore_signal(
            barrier, inc=1, device_id={"dp": lax.rem(me_dp + hop, groups)}, device_id_type=MESH
        )
    pl.semaphore_wait(barrier, n - 1 + groups - 1)

    def slot_of(ch, t):
        if ch is None:
            return mg.at[t]
        return xt.at[place(ch - 1)[2], t]

    def both(ch, action):
        @pl.when(ch == 0)
        def _():
            action(None, 0)

        @pl.when(jnp.logical_and(ch >= 1, ch <= B))
        def _():
            action(ch, ch)

    def own_copies(which, sem):
        if which is None:
            src = mg.at[me]
        else:
            src = noisy.at[place(which - 1)[2]]
        dst = slot_of(which, me)
        rsem = ag_recv.at[sem, me]
        return [
            (has_right, remote(src, dst, ag_send.at[sem, 0], rsem, right)),
            (has_left, remote(src, dst, ag_send.at[sem, 1], rsem, left)),
            (None, remote(src, dst, ag_send.at[sem, 2], rsem, partner)),
        ]

    def run(condition, action):
        if condition is None:
            action()
        else:
            pl.when(condition)(action)

    def send_own(which, sem):
        for condition, copy in own_copies(which, sem):
            run(condition, copy.start)

    def wait_own(which, sem):
        for condition, copy in own_copies(which, sem):
            run(condition, copy.wait_send)

    def hop_copies(which, sem, side, hop):
        source = (z - hop if side == 0 else z + hop) * 2 + c
        slot = slot_of(which, source)
        rsem = ag_recv.at[sem, source]
        base = 3 + (side * (nz - 1) + hop - 1) * 2
        onward = remote(slot, slot, ag_send.at[sem, base], rsem, right if side == 0 else left)
        across = remote(slot, slot, ag_send.at[sem, base + 1], rsem, partner)
        return onward, across

    def hop_exists(side, hop):
        return z >= hop if side == 0 else z + hop < nz

    def relay(which, sem, hop):
        for side in range(2):

            @pl.when(hop_exists(side, hop))
            def _(side=side):
                onward, across = hop_copies(which, sem, side, hop)
                across.wait_recv()
                run(has_right if side == 0 else has_left, onward.start)
                across.start()

    def wait_relay(which, sem, hop):
        for side in range(2):

            @pl.when(hop_exists(side, hop))
            def _(side=side):
                onward, across = hop_copies(which, sem, side, hop)
                run(has_right if side == 0 else has_left, onward.wait_send)
                across.wait_send()

    def wait_partner(which, sem):
        for other in range(nz):
            source = 2 * other + 1 - c
            slot = slot_of(which, source)
            remote(slot, slot, ag_send.at[sem, 2], ag_recv.at[sem, source], partner).wait_recv()

    for ch in range(1, 3):
        send_own(jnp.int32(ch), ch)
    for hop in range(1, groups):
        peer = lax.rem(me_dp + hop, groups)
        remote_dp(
            act_s, out_act.at[me_dp], dp_ssem.at[0, hop - 1], dp_rsem.at[0, hop - 1], peer
        ).start()
    own_act = pltpu.make_async_copy(act_s, out_act.at[me_dp], own_sem.at[0])
    own_act.start()
    own_rows = pltpu.make_async_copy(noisy, xt.at[:, me], own_sem.at[1])
    own_rows.start()

    rows_tmp[...] = jnp.zeros_like(rows_tmp)
    for kind in range(3):
        start = kind * 3 * B
        rows_tmp[start : start + B, :wp] = dot_nn(act_s[...], ada_s[kind])
        rows_tmp[start + B : start + 3 * B, :wp] = dot_nn(act_t[...], ada_t[kind])
    mg[me] = rows_tmp[...].T[:wp]
    send_own(None, 0)
    gq[...] = jnp.zeros_like(gq)
    go[...] = jnp.zeros_like(go)
    own_rows.wait()

    def mod_row(kind, model, b, cols):
        return mr[pl.ds((kind * 3 + model) * B + b, 1), cols]

    def forward(k):
        ch = k + 1
        wait_partner(ch, ch)
        b = place(k)[2]
        total = jnp.zeros((1, L), F32)
        square = jnp.zeros((1, L), F32)
        for t in range(n):
            values = xt[b, t].astype(F32)
            total += jnp.sum(values, axis=0, keepdims=True)
            square += jnp.sum(values * values, axis=0, keepdims=True)
        mean = total / D
        inv = lax.rsqrt(square / D - mean * mean + norm_eps)
        picked = [
            mod_row(kind, model, b, slice(None)) for kind in range(2) for model in range(3)
        ]
        colbuf[...] = jnp.concatenate(picked + picked[:2], axis=0).T
        for t in range(0, n, 2):
            rows = slice(t * wp, (t + 2) * wp)
            values = jnp.concatenate([xt[b, t].astype(F32), xt[b, t + 1].astype(F32)], axis=0)
            low = ((values - mean) * inv).astype(BF16)
            nt[b, rows, :] = low
            wide = low.astype(F32)
            for model in range(3):
                scale = colbuf[rows, 3 + model : 4 + model]
                shift = colbuf[rows, model : model + 1]
                md[model, rows, :] = (wide * (1.0 + scale) + shift).astype(BF16)
        mixed_all = []
        for model in range(3):
            weight = wq_s if model == 0 else wq_t
            qkv = dot_nn(weight[...], md[model])
            for h in range(heads):
                parts = [
                    qkv[(h * 3 + j) * HD : (h * 3 + j + 1) * HD].astype(BF16) for j in range(3)
                ]
                scores = dot_tn(parts[1], parts[0])
                top = jnp.max(scores, axis=0, keepdims=True)
                exponent = jnp.exp2((scores - top) * soft)
                inverse = 1.0 / jnp.sum(exponent, axis=0, keepdims=True)
                low = exponent.astype(BF16)
                mixed_all.append(dot_nn(parts[2], low) * inverse)
                if model == 0:
                    for j in range(3):
                        qs[b, h * 3 + j] = parts[j]
                    et[b, h] = low
                    rinv[b, h] = inverse
        ms[b] = jnp.concatenate(mixed_all[:heads], axis=0).astype(BF16)
        mx[...] = jnp.concatenate(mixed_all, axis=0).astype(BF16)
        power = strength[pl.ds(b, 1), :][:, :1]
        for cols in col_chunks:
            gate = [mod_row(2, model, b, cols) for model in range(3)]
            teacher = wo_t[:, cols].astype(F32)
            weights = jnp.concatenate(
                [
                    wo_s[:, cols].astype(F32) * (scale_norm * gate[0]),
                    teacher * ((-scale_norm * (1.0 + power)) * gate[1]),
                    teacher * ((scale_norm * power) * gate[2]),
                ],
                axis=0,
            ).astype(BF16)
            psend[b, :, cols] = dot_tn(mx[...], weights).astype(BF16)
        zo, co, _ = place(k)

        @pl.when(co != c)
        def _():
            part_copy(k).start()

    def part_copy(k):
        zo, co, b = place(k)
        return remote(psend.at[b], ppart.at[zo], pt_send.at[zo], pt_recv.at[zo], partner)

    def down_copy(zo):
        to_right = z < zo
        return (
            to_right,
            remote(psum.at[zo], pleft.at[zo], up_send.at[zo], left_recv.at[zo], right),
            remote(psum.at[zo], pright.at[zo], up_send.at[zo], right_recv.at[zo], left),
        )

    def gp_copies(b):
        slot = gp.at[b]
        rsem = gp_recv.at[b]
        return (
            remote(slot, slot, gp_send.at[b, 0], rsem, right),
            remote(slot, slot, gp_send.at[b, 1], rsem, left),
            remote(slot, slot, gp_send.at[b, 2], rsem, partner),
        )

    def chain_place(zo):
        longest = jnp.maximum(zo, nz - 1 - zo)
        return jnp.where(z < zo, z, jnp.where(z > zo, nz - 1 - z, longest))

    row_step = 64 if L % 64 == 0 else L

    def reduce_chain(k):
        zo, co, b = place(k)
        part_copy(k).wait_recv()
        _, rightward, leftward = down_copy(zo)
        from_left = jnp.logical_and(has_left, z <= zo)
        from_right = jnp.logical_and(has_right, z >= zo)

        @pl.when(from_left)
        def _():
            rightward.wait_recv()

        @pl.when(from_right)
        def _():
            leftward.wait_recv()

        def add(dst, sources):
            for start in range(0, L, row_step):
                rows = pl.ds(start, row_step)
                value = sources[0][rows, :].astype(F32)
                for source in sources[1:]:
                    value += source[rows, :].astype(F32)
                dst[rows, :] = value.astype(BF16)

        base = [psend.at[b], ppart.at[zo]]
        owner = z == zo

        @pl.when(jnp.logical_not(owner))
        def _():
            none = jnp.logical_not(jnp.logical_or(from_left, from_right))
            pl.when(none)(lambda: add(psum.at[zo], base))
            pl.when(from_left)(lambda: add(psum.at[zo], base + [pleft.at[zo]]))
            pl.when(from_right)(lambda: add(psum.at[zo], base + [pright.at[zo]]))
            to_right, rightward, leftward = down_copy(zo)
            pl.when(to_right)(rightward.start)
            pl.when(jnp.logical_not(to_right))(leftward.start)

        @pl.when(owner)
        def _():
            two = jnp.logical_and(from_left, from_right)
            pl.when(two)(lambda: add(gp.at[b], base + [pleft.at[zo], pright.at[zo]]))
            pl.when(jnp.logical_not(from_right))(lambda: add(gp.at[b], base + [pleft.at[zo]]))
            pl.when(jnp.logical_not(from_left))(lambda: add(gp.at[b], base + [pright.at[zo]]))
            to_right, to_left, across = gp_copies(b)
            pl.when(has_right)(to_right.start)
            pl.when(has_left)(to_left.start)
            across.start()

    def spread(k):
        zo, co, b = place(k)
        to_right, to_left, across = gp_copies(b)
        across.wait_recv()
        pl.when(jnp.logical_and(z > zo, has_right))(to_right.start)
        pl.when(jnp.logical_and(z < zo, has_left))(to_left.start)
        across.start()

    def backward(k):
        zo, co, b = place(k)

        @pl.when(co != c)
        def _():
            gp_copies(b)[2].wait_recv()

        grad_low = jnp.zeros((hc, L), F32)
        for cols in col_chunks:
            gate = mod_row(2, 0, b, cols)
            low = gp[b, :, cols]
            weight = wo_s[:, cols].astype(F32)
            grad_low += dot_nt((weight * gate).astype(BF16), low)
            outer = dot_nn(ms[b], low)
            go[:, cols] += outer * gate
            gm[pl.ds(b * 3 + 2, 1), cols] = jnp.sum(weight * outer, axis=0, keepdims=True)
        grads = []
        for h in range(heads):
            queries, keys, values = [qs[b, h * 3 + j] for j in range(3)]
            exponent = et[b, h]
            inverse = rinv[b, h]
            rows = grad_low[h * HD : (h + 1) * HD].astype(BF16)
            probs_grad = dot_tn(values, rows)
            wide = exponent.astype(F32)
            delta = jnp.sum(wide * probs_grad, axis=0, keepdims=True) * inverse
            score_grad = (
                wide * (probs_grad - delta) * (inverse * (1.0 / math.sqrt(HD)))
            ).astype(BF16)
            grads.append(dot_nn(keys, score_grad))
            grads.append(dot_nt(queries, score_grad))
            grads.append(dot_nt((rows.astype(F32) * inverse).astype(BF16), exponent))
        act_grad = jnp.concatenate(grads, axis=0).astype(BF16)
        over_tokens = jnp.sum(act_grad.astype(F32), axis=1, keepdims=True)
        for cols in col_chunks:
            product = dot_nt(act_grad, nt[b, cols, :])
            weight = wq_s[:, cols].astype(F32)
            gm[pl.ds(b * 3, 1), cols] = jnp.sum(weight * over_tokens, axis=0, keepdims=True)
            gm[pl.ds(b * 3 + 1, 1), cols] = jnp.sum(weight * product, axis=0, keepdims=True)
            gq[:, cols] += product * (1.0 + mod_row(1, 0, b, cols)) + over_tokens * mod_row(
                0, 0, b, cols
            )

    def valid(k):
        return jnp.logical_and(k >= 0, k < B)

    def step(s, carry):
        @pl.when(s + 3 <= B)
        def _():
            send_own(s + 3, s + 3)

        for hop in range(1, nz):
            both(s - hop + 1, lambda which, sem, hop=hop: relay(which, sem, hop))

        def chain(p, inner):
            k = s - first_sum - p
            zo, co, b = place(k)
            mine = jnp.logical_and(co == c, chain_place(zo) == p)

            @pl.when(jnp.logical_and(valid(k), mine))
            def _():
                reduce_chain(k)

            return inner

        lax.fori_loop(0, nz, chain, 0)

        def spreads(q, inner):
            k = s - first_sum - q
            zo, co, b = place(k)
            longest = jnp.maximum(zo, nz - 1 - zo)
            away = jnp.abs(z - zo)
            mine = jnp.logical_and(co == c, jnp.logical_and(away > 0, longest + away == q))

            @pl.when(jnp.logical_and(valid(k), mine))
            def _():
                spread(k)

            return inner

        lax.fori_loop(1, 2 * nz - 1, spreads, 0)

        @pl.when(s == first_fwd)
        def _():
            wait_partner(None, 0)
            mr[...] = jnp.concatenate([mg[t] for t in range(n)], axis=0).T

        @pl.when(valid(s - first_fwd))
        def _():
            forward(s - first_fwd)

        @pl.when(valid(s - first_bwd))
        def _():
            backward(s - first_bwd)

        return carry

    lax.fori_loop(0, B + first_bwd, step, 0)

    mod_copies = []
    for t in range(n):
        mt_send[t] = gm[:, t * wp : (t + 1) * wp]
    for hop in range(1, n):
        peer = lax.rem(me + hop, n)
        mod_copies.append(
            remote(
                mt_send.at[peer],
                mt_land.at[hop - 1],
                mt_ssem.at[hop - 1],
                mt_rsem.at[hop - 1],
                peer,
            )
        )
        mod_copies[-1].start()

    for cols in col_chunks:
        gqt[cols, :] = gq[:, cols].T
    grad_copies = []
    for g in range(groups):
        qk_send[g] = gqt[g * depth : (g + 1) * depth, :].astype(BF16)
        go_send[g] = go[:, g * depth : (g + 1) * depth].astype(BF16)
    for hop in range(1, groups):
        peer = lax.rem(me_dp + hop, groups)
        for index, (src, dst) in enumerate([(qk_send, qk_land), (go_send, go_land)]):
            grad_copies.append(
                remote_dp(
                    src.at[peer],
                    dst.at[hop - 1],
                    dp_ssem.at[1 + index, hop - 1],
                    dp_rsem.at[1 + index, hop - 1],
                    peer,
                )
            )
            grad_copies[-1].start()

    for copy in mod_copies:
        copy.wait_recv()
    own_mod = mt_send[me]
    for hop in range(1, n):
        own_mod += mt_land[hop - 1]
    out_mod[me_dp] = own_mod
    for hop in range(1, groups):
        peer = lax.rem(me_dp + hop, groups)
        copy = remote_dp(
            out_mod.at[me_dp],
            out_mod.at[me_dp],
            dp_ssem.at[3, hop - 1],
            dp_rsem.at[3, hop - 1],
            peer,
        )
        copy.start()
        grad_copies.append(copy)

    def drain(ch, carry):
        both(ch, lambda which, sem: wait_own(which, sem))
        for hop in range(1, nz):
            both(ch, lambda which, sem, hop=hop: wait_relay(which, sem, hop))
        return carry

    lax.fori_loop(0, B + 1, drain, 0)

    def drain_sums(k, carry):
        zo, co, b = place(k)

        @pl.when(co != c)
        def _():
            part_copy(k).wait_send()

        @pl.when(co == c)
        def _():
            to_right, rightward, leftward = down_copy(zo)
            pl.when(z != zo)(rightward.wait_send)
            right_copy, left_copy, across = gp_copies(b)
            pl.when(jnp.logical_and(z >= zo, has_right))(right_copy.wait_send)
            pl.when(jnp.logical_and(z <= zo, has_left))(left_copy.wait_send)
            across.wait_send()

        return carry

    lax.fori_loop(0, B, drain_sums, 0)
    for copy in mod_copies:
        copy.wait_send()
    for hop in range(1, groups):
        peer = lax.rem(me_dp + hop, groups)
        remote_dp(
            act_s, out_act.at[me_dp], dp_ssem.at[0, hop - 1], dp_rsem.at[0, hop - 1], peer
        ).wait()
    own_act.wait()
    for copy in grad_copies:
        copy.wait()
    grad_qkv = qk_send[me_dp].astype(F32)
    grad_out = go_send[me_dp].astype(F32)
    for hop in range(1, groups):
        grad_qkv += qk_land[hop - 1].astype(F32)
        grad_out += go_land[hop - 1].astype(F32)
    out_qkv[...] = grad_qkv
    out_go[...] = grad_out


def round_up(value, unit):
    return (value + unit - 1) // unit * unit


def run_step(noisy_t, act_s, act_t, strength, ada_s, ada_t, wq_s, wq_t, wo_s, wo_t):
    n = lax.axis_size("tensor")
    groups = lax.axis_size("dp")
    B, wp, L = noisy_t.shape
    D = wp * n
    hc = wo_s.shape[0]
    heads = hc // HD
    nz = n // 2
    depth = D // groups
    assert B <= n and n % 4 == 0
    lanes = round_up(9 * B, 128)
    scale_norm = 1.0 / math.sqrt(B * groups * L)
    sizes = (B, L, D, n, groups, heads, scale_norm)
    operands = (noisy_t, act_s, act_t, strength, ada_s, ada_t, wq_s, wq_t, wo_s, wo_t)
    dma = pltpu.SemaphoreType.DMA
    vmem = pltpu.VMEM
    scratch = [
        vmem((B, n, wp, L), BF16),
        vmem((n, wp, lanes), F32),
        vmem((lanes, D), F32),
        vmem((lanes, round_up(wp, 128)), F32),
        vmem((D, 8), F32),
        vmem((B, D, L), BF16),
        vmem((3, D, L), BF16),
        vmem((B, heads * 3, HD, L), BF16),
        vmem((B, heads, L, L), BF16),
        vmem((B, heads, 1, L), F32),
        vmem((B, hc, L), BF16),
        vmem((3 * hc, L), BF16),
        vmem((B, L, D), BF16),
        vmem((nz, L, D), BF16),
        vmem((nz, L, D), BF16),
        vmem((nz, L, D), BF16),
        vmem((nz, L, D), BF16),
        vmem((B, L, D), BF16),
        vmem((3 * hc, D), F32),
        vmem((hc, D), F32),
        vmem((3 * B, D), F32),
        vmem((n, 3 * B, wp), F32),
        vmem((n - 1, 3 * B, wp), F32),
        vmem((D, 3 * hc), F32),
        vmem((groups, depth, 3 * hc), BF16),
        vmem((groups - 1, depth, 3 * hc), BF16),
        vmem((groups, hc, depth), BF16),
        vmem((groups - 1, hc, depth), BF16),
        dma((B + 1, 3 + 4 * (nz - 1))),
        dma((B + 1, n)),
        dma((nz,)),
        dma((nz,)),
        dma((nz,)),
        dma((nz,)),
        dma((nz,)),
        dma((B, 3)),
        dma((B,)),
        dma((n - 1,)),
        dma((n - 1,)),
        dma((4, groups - 1)),
        dma((4, groups - 1)),
        dma((2,)),
    ]
    return pl.pallas_call(
        functools.partial(step_kernel, sizes),
        out_shape=[
            jax.ShapeDtypeStruct((depth, 3 * hc), F32),
            jax.ShapeDtypeStruct((hc, depth), F32),
            jax.ShapeDtypeStruct((groups, 3 * B, wp), F32),
            jax.ShapeDtypeStruct((groups, B, D), BF16),
        ],
        in_specs=[pl.BlockSpec(memory_space=pltpu.VMEM)] * len(operands),
        out_specs=[pl.BlockSpec(memory_space=pltpu.VMEM)] * 4,
        scratch_shapes=scratch,
        compiler_params=pltpu.CompilerParams(
            collective_id=0, has_side_effects=True, vmem_limit_bytes=62 * 1024 * 1024
        ),
    )(*operands)


def local(
    noisy,
    labels,
    tsteps,
    guide_index,
    class_table,
    time_table,
    guide_table,
    guide_weights,
    teacher_qkv,
    teacher_out,
    teacher_ada,
    student_qkv,
    student_out,
    student_ada,
):
    samples, seq_len, width_part = noisy.shape
    groups = lax.axis_size("dp")
    null_class = class_table.shape[0] - 1
    time_embed = lookup_rows(tsteps, time_table)
    cond_embed = lookup_rows(labels, class_table) + time_embed
    null_embed = class_table[null_class].astype(F32)[None, :] + time_embed
    guide_hot = guide_index[:, None] == jnp.arange(guide_table.shape[0], dtype=jnp.int32)[None, :]
    student_embed = cond_embed + jnp.dot(
        guide_hot.astype(BF16), guide_table, preferred_element_type=F32
    )
    strength = jnp.sum(jnp.where(guide_hot, guide_weights[None, :], 0.0), axis=1)
    cond_act = jax.nn.silu(cond_embed).astype(BF16)
    null_act = jax.nn.silu(null_embed).astype(BF16)
    student_act = jax.nn.silu(student_embed).astype(BF16)
    teacher_act = jnp.concatenate([cond_act, null_act], axis=0)
    grad_qkv, grad_out, wide_grad, act_all = run_step(
        noisy.transpose(0, 2, 1),
        student_act,
        teacher_act,
        jnp.broadcast_to(strength[:, None], (samples, 128)),
        student_ada,
        teacher_ada,
        student_qkv.T,
        teacher_qkv.T,
        student_out,
        teacher_out,
    )
    model_width = act_all.shape[2]
    depth = model_width // groups
    own_act = lax.dynamic_slice_in_dim(act_all, lax.axis_index("dp") * depth, depth, axis=2)
    grad_ada = jnp.einsum(
        "bd,bke->kde",
        own_act.reshape(samples * groups, depth).astype(F32),
        wide_grad.reshape(samples * groups, 3, width_part),
        precision=lax.Precision.HIGHEST,
    )
    return (grad_qkv, grad_out, grad_ada)


def solution(mesh):
    return jax.shard_map(
        local,
        mesh=mesh,
        in_specs=(
            P("dp", None, "tensor"),
            P("dp"),
            P("dp"),
            P("dp"),
            P(),
            P(),
            P(),
            P(),
            P(None, "tensor"),
            P("tensor", None),
            P(None, None, "tensor"),
            P(None, "tensor"),
            P("tensor", None),
            P(None, None, "tensor"),
        ),
        out_specs=(P("dp", "tensor"), P("tensor", "dp"), P(None, "dp", "tensor")),
        check_vma=False,
    )
```

time: 301 us -> 187 us (0.62)
  matrix products: 56.5 us -> 5.61 us
  Pallas kernels: 123 us -> 171 us
  waiting for transfers between devices: 29.4 us -> 0 us
  other arithmetic: 28.6 us -> 1.72 us
  blocking collectives: 20.1 us -> 0 us
  local copies, waits for them, and re-layouts: 27.3 us -> 7.74 us
  between operations: 15 us -> 0.73 us
    dot_general x20 -> x4, matrix products: 56.5 us -> 5.61 us  [the longest x2 2.68 us: lookup_rows(): return jnp.dot(one_hot, table_rows, preferred_element_type=F32)]
    pallas_call x5 -> x1, Pallas kernels: 123 us -> 171 us  [run_step(): pl.pallas_call(functools.partial(step_kernel, sizes), out_shape=[jax.Shap...]
    all_gather x3 -> x0, waiting for transfers between devices: 28 us -> none  [the longest x1 27.9 us: local(): wide_noisy = lax.all_gather(noisy, 'tensor', axis=2, tiled=True)]
    all_gather x1 -> x0, blocking collectives: 20.1 us -> none  [gather_mods(): gathered = lax.all_gather(mods, 'tensor', axis=0)]
    reduce_sum x4 -> x0, other arithmetic: 9.77 us -> none  [the longest x1 4.1 us: local(): row_mean = jnp.sum(signal, axis=2, keepdims=True) / model_width]
    sub x2 -> x0, other arithmetic: 9.56 us -> none  [attend(): exponent = jnp.exp(scores - jnp.max(scores, axis=-1, keepdims=True))]
    all_gather x1 -> x0, local copies, waits for them, and re-layouts: 7.04 us -> none  [local(): wide_noisy = lax.all_gather(noisy, 'tensor', axis=2, tiled=True)]
    convert_element_type x3 -> x0, other arithmetic: 5.85 us -> none  [the longest x1 4.49 us: modulate(): (normed.astype(jnp.float32) * (1.0 + scale[:, None]) + shift[:, None]).as...]
  transfers between devices with their start and end apart: 4 -> 0, of which waited for: 1 -> 0; matrix products, arithmetic and copies ran while one was open for 29% -> 0% of each run, Pallas kernels for 24% -> 0%
where the time goes in v1:
time: 187 us
  Pallas kernels  171 us (91%)
  local copies, waits for them, and re-layouts  7.74 us (4%)
  matrix products  5.61 us (3%)
    pallas_call x1, Pallas kernels, run_step(): pl.pallas_call(functools.partial(step_kernel, sizes), out_shape=[jax.Shap...  171 us
    unnamed x20, local copies, waits for them, and re-layouts  6.1 us

profile of v1, /device:TPU:0, one launch (start us, length us, event | category | flops | bytes accessed | tf_op | source)
XLA Modules:
  0.0 187.2 jit_solution(2166204056748443233)
XLA Ops:
  0.6 0.0 copy-start
  0.6 0.0 copy-start.1
  0.7 0.0 copy-start.5
  0.7 0.9 convert_reduce_fusion
  1.6 0.0 copy-start.6
  1.6 0.0 copy-start.2
  1.6 2.2 %multiply_convert_fusion = (bf16[8,1152]{1,0:T(8,128)(2,1)S(1)}, f32[8,1152]{1,0:T(8,128)S(1)}) fusion(f32[1152]{0:T(1024)S(1)} %convert_reduce_fusion, bf16[1000,1152]{1,0:T(8,128)(2,1)} %param.19, s32[8]{0:T(128)} %param.16), kind=kOutput, calls=%fused_computation.5 | convolution fusion | flops 18495296 | bytes 2363936 | tf_op jit(solution)/shard_map/dot_general | solution.py:24
  3.8 0.0 copy-done.1
  3.8 0.0 copy-done.5
  3.8 0.0 copy-start.3
  3.8 0.5 multiply_convert_fusion.1
  4.3 0.6 pad_maximum_fusion.act_t
  4.9 0.0 copy-done.6
  4.9 0.8 multiply_convert_fusion.2.act_s
  5.8 1.7 copy.23.ada_s
  7.5 1.7 copy.24.ada_t
  9.2 0.2 select_reduce_fusion
  9.4 0.7 broadcast_in_dim.16.strength
  10.1 171.4 %shard_map.157 = (f32[288,432]{1,0:T(8,128)}, f32[144,288]{1,0:T(8,128)}, f32[4,24,144]{2,1,0:T(8,128)}, bf16[4,8,1152]{2,1,0:T(8,128)(2,1)}) custom-call(bf16[8,144,256]{2,1,0:T(8,128)(2,1)} %bitcast.15, bf16[8,1152]{1,0:T(8,128)(2,1)} %multiply_convert_fusion.2.act_s, bf16[16,1152]{1,0:T(8,128)(2,1)} %pad_maximum_fusion.act_t, ...), custom_call_target="tpu_custom_call" | custom-call | tf_op jit(solution)/shard_map/pallas_call | solution.py:671
  181.5 1.0 reshape.17
  182.5 2.1 %convolution_bitcast_fusion = f32[3,288,144]{1,2,0:T(8,128)} fusion(f32[32,3,144]{2,1,0:T(4,128)S(1)} %reshape.17, bf16[4,8,1152]{2,1,0:T(8,128)(2,1)} %get-tuple-element.10, s32[]{:T(128)S(6)} %select_n.8), kind=kOutput, calls=%fused_computation.2 | convolution fusion | flops 47775744 | bytes 577540 | tf_op jit(solution)/shard_map/bd,bke->kde/dot_general | solution.py:734
  184.6 1.9 %copy.30 = f32[288,432]{1,0:T(8,128)} copy(f32[288,432]{1,0:T(8,128)} %get-tuple-element.18) | data formatting | bytes 995328
  186.5 0.0 copy-done.4
  186.5 0.7 copy.31
  (6 shorter events, 0.0 us)
Async XLA Ops:
  0.6 4.3 %copy-start = (bf16[32,1152]{1,0:T(8,128)(2,1)S(1)}, bf16[32,1152]{1,0:T(8,128)(2,1)}, u32[]{:S(2)}) copy-start(bf16[32,1152]{1,0:T(8,128)(2,1)} %param.20) | copy-start | bytes 221188
  0.6 3.2 %copy-start.1 = (bf16[1001,1152]{1,0:T(8,128)(2,1)S(1)}, bf16[1001,1152]{1,0:T(8,128)(2,1)}, u32[]{:S(2)}) copy-start(bf16[1001,1152]{1,0:T(8,128)(2,1)} %param.18) | copy-start | bytes 6918916
  0.7 3.2 %copy-start.5 = (s32[8]{0:T(128)S(1)}, s32[8]{0:T(128)}, u32[]{:S(2)}) copy-start(s32[8]{0:T(128)} %param.15) | copy-start | bytes 100
  1.6 3.4 %copy-start.6 = (s32[8]{0:T(128)S(1)}, s32[8]{0:T(128)}, u32[]{:S(2)}) copy-start(s32[8]{0:T(128)} %param.17) | copy-start | bytes 100
  1.6 4.2 %copy-start.2 = (bf16[3,1152,144]{1,2,0:T(8,128)(2,1)S(1)}, bf16[3,1152,144]{1,2,0:T(8,128)(2,1)}, u32[]{:S(2)}) copy-start(bf16[3,1152,144]{1,2,0:T(8,128)(2,1)} %param.27) | copy-start | bytes 2985988
  3.8 3.7 %copy-start.3 = (bf16[3,1152,144]{1,2,0:T(8,128)(2,1)S(1)}, bf16[3,1152,144]{1,2,0:T(8,128)(2,1)}, u32[]{:S(2)}) copy-start(bf16[3,1152,144]{1,2,0:T(8,128)(2,1)} %param.24) | copy-start | bytes 2985988
  5.8 3.5 %copy-start.7 = (f32[32]{0:T(128)S(1)}, f32[32]{0:T(128)}, u32[]{:S(2)}) copy-start(f32[32]{0:T(128)} %param.21) | copy-start | bytes 388
  181.5 5.0 %copy-start.4 = (f32[144,288]{1,0:T(8,128)S(1)}, f32[144,288]{1,0:T(8,128)}, u32[]{:S(2)}) copy-start(f32[144,288]{1,0:T(8,128)} %get-tuple-element.19) | copy-start | bytes 497668

commit v2 on v1

v2 whole, which is shorter than its diff:
```python
import functools
import math

import jax
import jax.numpy as jnp
from jax import lax
from jax.experimental import pallas as pl
from jax.experimental.pallas import tpu as pltpu
from jax.sharding import PartitionSpec as P

HD = 72
MESH = pl.DeviceIdType.MESH
F32 = jnp.float32
BF16 = jnp.bfloat16

norm_eps = 1e-06
LOG2E = math.log2(math.e)
SUBS = 2
CHAIN_GAP = 2


def dot_nn(a, b):
    return lax.dot_general(a, b, (((1,), (0,)), ((), ())), preferred_element_type=F32)


def dot_tn(a, b):
    return lax.dot_general(a, b, (((0,), (0,)), ((), ())), preferred_element_type=F32)


def dot_nt(a, b):
    return lax.dot_general(a, b, (((1,), (1,)), ((), ())), preferred_element_type=F32)


def step_kernel(
    sizes,
    labels,
    tsteps,
    guide_index,
    guide_weights,
    noisy,
    guide_table,
    class_hbm,
    time_hbm,
    ada_s_hbm,
    ada_t_hbm,
    wq_s_hbm,
    wq_t_hbm,
    wo_s_hbm,
    wo_t_hbm,
    out_qkv,
    out_go,
    out_ada,
    class_table,
    time_table,
    ada_s,
    ada_t,
    wq_s,
    wq_t,
    wo_s,
    wo_t,
    strength,
    act_s,
    act_t,
    act_send,
    act_land,
    mod_land,
    xt,
    mg,
    mr,
    colbuf,
    nt,
    md,
    qs,
    et,
    rinv,
    ms,
    mx,
    psend,
    ppart,
    pleft,
    pright,
    psum,
    gp,
    acc,
    gm,
    mt_send,
    mt_land,
    grad_send,
    grad_land,
    ag_send,
    ag_recv,
    pt_send,
    pt_recv,
    up_send,
    left_recv,
    right_recv,
    gp_send,
    gp_recv,
    mt_ssem,
    mt_rsem,
    dp_ssem,
    dp_rsem,
    own_sem,
    load_sem,
):
    B, L, D, n, groups, heads, scale_norm = sizes
    nz = n // 2
    wp = D // n
    hc = heads * HD
    depth = D // groups
    chunk = 384 if D % 384 == 0 else 128
    col_chunks = [pl.ds(start, chunk) for start in range(0, D, chunk)]
    me = lax.axis_index("tensor")
    me_dp = lax.axis_index("dp")
    z = lax.div(me, 2)
    c = lax.rem(me, 2)
    partner = 2 * z + (1 - c)
    right = lax.rem(me + 2, n)
    left = lax.rem(me + n - 2, n)
    has_left = z > 0
    has_right = z < nz - 1
    first_fwd = nz
    first_sum = nz + 1
    reach = nz // 2
    first_spread = first_sum + CHAIN_GAP * reach
    first_bwd = first_spread + reach + 1
    soft = LOG2E / math.sqrt(HD)
    subs = SUBS
    row_step = L // subs

    def remote(src, dst, ssem, rsem, target):
        return pltpu.make_async_remote_copy(
            src_ref=src,
            dst_ref=dst,
            send_sem=ssem,
            recv_sem=rsem,
            device_id={"tensor": target},
            device_id_type=MESH,
        )

    def remote_dp(src, dst, ssem, rsem, target):
        return pltpu.make_async_remote_copy(
            src_ref=src,
            dst_ref=dst,
            send_sem=ssem,
            recv_sem=rsem,
            device_id={"dp": target},
            device_id_type=MESH,
        )

    def place(k):
        four = lax.div(k, 4)
        item = k - 4 * four
        return reach - 1 + lax.rem(item, 2), lax.div(item, 2), k

    def seat(k):
        return 2 * lax.div(k, 4) + lax.rem(k, 2)

    loads = [
        pltpu.make_async_copy(src, dst, load_sem.at[index])
        for index, (src, dst) in enumerate(
            [
                (class_hbm, class_table),
                (time_hbm, time_table),
                (ada_s_hbm, ada_s),
                (ada_t_hbm, ada_t),
                (wq_s_hbm, wq_s),
                (wq_t_hbm, wq_t),
                (wo_s_hbm, wo_s),
                (wo_t_hbm, wo_t),
            ]
        )
    ]
    for load in loads:
        load.start()
    barrier = pltpu.get_barrier_semaphore()
    for hop in range(1, n):
        pl.semaphore_signal(
            barrier, inc=1, device_id={"tensor": lax.rem(me + hop, n)}, device_id_type=MESH
        )
    for hop in range(1, groups):
        pl.semaphore_signal(
            barrier, inc=1, device_id={"dp": lax.rem(me_dp + hop, groups)}, device_id_type=MESH
        )
    pl.semaphore_wait(barrier, n - 1 + groups - 1)

    def slot_of(ch, t):
        if ch is None:
            return mg.at[t]
        return xt.at[place(ch - 1)[2], t]

    def both(ch, action):
        @pl.when(ch == 0)
        def _():
            action(None, 0)

        @pl.when(jnp.logical_and(ch >= 1, ch <= B))
        def _():
            action(ch, ch)

    def own_copies(which, sem):
        if which is None:
            src = mg.at[me]
        else:
            src = noisy.at[place(which - 1)[2]]
        dst = slot_of(which, me)
        rsem = ag_recv.at[sem, me]
        return [
            (has_right, remote(src, dst, ag_send.at[sem, 0], rsem, right)),
            (has_left, remote(src, dst, ag_send.at[sem, 1], rsem, left)),
            (None, remote(src, dst, ag_send.at[sem, 2], rsem, partner)),
        ]

    def run(condition, action):
        if condition is None:
            action()
        else:
            pl.when(condition)(action)

    def send_own(which, sem):
        for condition, copy in own_copies(which, sem):
            run(condition, copy.start)

    def wait_own(which, sem):
        for condition, copy in own_copies(which, sem):
            run(condition, copy.wait_send)

    def hop_copies(which, sem, side, hop):
        source = (z - hop if side == 0 else z + hop) * 2 + c
        slot = slot_of(which, source)
        rsem = ag_recv.at[sem, source]
        base = 3 + (side * (nz - 1) + hop - 1) * 2
        onward = remote(slot, slot, ag_send.at[sem, base], rsem, right if side == 0 else left)
        across = remote(slot, slot, ag_send.at[sem, base + 1], rsem, partner)
        return onward, across

    def hop_exists(side, hop):
        return z >= hop if side == 0 else z + hop < nz

    def relay(which, sem, hop):
        for side in range(2):

            @pl.when(hop_exists(side, hop))
            def _(side=side):
                onward, across = hop_copies(which, sem, side, hop)
                across.wait_recv()
                run(has_right if side == 0 else has_left, onward.start)
                across.start()

    def wait_relay(which, sem, hop):
        for side in range(2):

            @pl.when(hop_exists(side, hop))
            def _(side=side):
                onward, across = hop_copies(which, sem, side, hop)
                run(has_right if side == 0 else has_left, onward.wait_send)
                across.wait_send()

    def wait_partner(which, sem):
        for other in range(nz):
            source = 2 * other + 1 - c
            slot = slot_of(which, source)
            remote(slot, slot, ag_send.at[sem, 2], ag_recv.at[sem, source], partner).wait_recv()

    for ch in range(1, 3):
        send_own(jnp.int32(ch), ch)
    own_rows = pltpu.make_async_copy(noisy, xt.at[:, me], own_sem.at[0])
    own_rows.start()
    acc[...] = jnp.zeros_like(acc)
    mg[me] = jnp.zeros_like(mg[me])
    for load in loads[:2]:
        load.wait()

    def silu(value):
        return value / (1.0 + jnp.exp(-value))

    def lookup(table, indices):
        count = table.shape[0]
        even = count // 16 * 16
        spots = lax.broadcasted_iota(jnp.int32, (B, even), 1)
        found = dot_nn((spots == indices[...]).astype(F32).astype(BF16), table[:even, :])
        for row in range(even, count):
            found += jnp.where(indices[...] == row, table[row : row + 1, :].astype(F32), 0.0)
        return found

    last = class_table.shape[0] - 1
    time_embed = lookup(time_table, tsteps)
    cond_embed = lookup(class_table, labels) + time_embed
    null_embed = class_table[last : last + 1, :].astype(F32) + time_embed
    student_embed = cond_embed + lookup(guide_table, guide_index)
    act_s[...] = silu(student_embed).astype(BF16)
    act_t[...] = silu(jnp.concatenate([cond_embed, null_embed], axis=0)).astype(BF16)
    guides = guide_weights.shape[1]
    guide_spots = lax.broadcasted_iota(jnp.int32, (B, guides), 1) == guide_index[...]
    strength[...] = jnp.broadcast_to(
        jnp.sum(jnp.where(guide_spots, guide_weights[...], 0.0), axis=1, keepdims=True), (B, 128)
    )
    for load in loads[2:]:
        load.wait()
    for kind in range(3):
        start = kind * 3 * B
        mg[me, :, start : start + B] = dot_nt(ada_s[kind], act_s[...])
        mg[me, :, start + B : start + 3 * B] = dot_nt(ada_t[kind], act_t[...])
    send_own(None, 0)
    for g in range(groups):
        act_send[g] = act_s[:, g * depth : (g + 1) * depth]
    act_copies = []
    for hop in range(1, groups):
        peer = lax.rem(me_dp + hop, groups)
        act_copies.append(
            remote_dp(
                act_send.at[peer],
                act_land.at[me_dp],
                dp_ssem.at[0, hop - 1],
                dp_rsem.at[0, hop - 1],
                peer,
            )
        )
        act_copies[-1].start()
    act_land[me_dp] = act_send[me_dp]
    own_rows.wait()

    def mod_row(kind, model, b, cols):
        return mr[pl.ds((kind * 3 + model) * B + b, 1), cols]

    def forward(k):
        ch = k + 1
        wait_partner(ch, ch)
        b = place(k)[2]
        total = jnp.zeros((1, L), F32)
        square = jnp.zeros((1, L), F32)
        for t in range(n):
            values = xt[b, t].astype(F32)
            total += jnp.sum(values, axis=0, keepdims=True)
            square += jnp.sum(values * values, axis=0, keepdims=True)
        mean = total / D
        inv = lax.rsqrt(square / D - mean * mean + norm_eps)
        picked = [
            mod_row(kind, model, b, slice(None)) for kind in range(2) for model in range(3)
        ]
        colbuf[...] = jnp.concatenate(picked + picked[:2], axis=0).T
        for t in range(0, n, 2):
            rows = slice(t * wp, (t + 2) * wp)
            values = jnp.concatenate([xt[b, t].astype(F32), xt[b, t + 1].astype(F32)], axis=0)
            low = ((values - mean) * inv).astype(BF16)
            nt[b, rows, :] = low
            wide = low.astype(F32)
            for model in range(3):
                scale = colbuf[rows, 3 + model : 4 + model]
                shift = colbuf[rows, model : model + 1]
                md[model, rows, :] = (wide * (1.0 + scale) + shift).astype(BF16)
        mixed_all = []
        for model in range(3):
            weight = wq_s if model == 0 else wq_t
            qkv = dot_nn(weight[...], md[model])
            for h in range(heads):
                parts = [
                    qkv[(h * 3 + j) * HD : (h * 3 + j + 1) * HD].astype(BF16) for j in range(3)
                ]
                scores = dot_tn(parts[1], parts[0])
                top = jnp.max(scores, axis=0, keepdims=True)
                exponent = jnp.exp2((scores - top) * soft)
                inverse = 1.0 / jnp.sum(exponent, axis=0, keepdims=True)
                low = exponent.astype(BF16)
                mixed_all.append(dot_nn(parts[2], low) * inverse)
                if model == 0:
                    for j in range(3):
                        qs[b, h * 3 + j] = parts[j]
                    et[b, h] = low
                    rinv[b, h] = inverse
        ms[b] = jnp.concatenate(mixed_all[:heads], axis=0).astype(BF16)
        mx[...] = jnp.concatenate(mixed_all, axis=0).astype(BF16)
        power = strength[pl.ds(b, 1), :][:, :1]
        for cols in col_chunks:
            gate = [mod_row(2, model, b, cols) for model in range(3)]
            teacher = wo_t[:, cols].astype(F32)
            weights = jnp.concatenate(
                [
                    wo_s[:, cols].astype(F32) * (scale_norm * gate[0]),
                    teacher * ((-scale_norm * (1.0 + power)) * gate[1]),
                    teacher * ((scale_norm * power) * gate[2]),
                ],
                axis=0,
            ).astype(BF16)
            psend[b, :, cols] = dot_tn(mx[...], weights).astype(BF16)
        zo, co, _ = place(k)

        @pl.when(co != c)
        def _():
            for sub in range(subs):
                part_copy(k, sub).start()

    def piece(ref, index, sub):
        start = sub * row_step
        if not isinstance(sub, int):
            start = pl.multiple_of(start, row_step)
        return ref.at[index, pl.ds(start, row_step)]

    def part_copy(k, sub):
        zo, co, b = place(k)
        return remote(
            piece(psend, b, sub),
            piece(ppart, seat(k), sub),
            pt_send.at[seat(k), sub],
            pt_recv.at[seat(k), sub],
            partner,
        )

    def down_copies(k, sub):
        index = seat(k)
        src = piece(psum, index, sub)
        ssem = up_send.at[index, sub]
        return (
            remote(src, piece(pleft, index, sub), ssem, left_recv.at[index, sub], right),
            remote(src, piece(pright, index, sub), ssem, right_recv.at[index, sub], left),
        )

    def gp_copies(b, sub):
        slot = piece(gp, b, sub)
        rsem = gp_recv.at[b, sub]
        return (
            remote(slot, slot, gp_send.at[b, sub, 0], rsem, right),
            remote(slot, slot, gp_send.at[b, sub, 1], rsem, left),
            remote(slot, slot, gp_send.at[b, sub, 2], rsem, partner),
        )

    def chain_place(zo):
        return jnp.where(z < zo, z, jnp.where(z > zo, nz - 1 - z, reach))

    def reduce_chain(k):
        zo, co, b = place(k)
        from_left = jnp.logical_and(has_left, z <= zo)
        from_right = jnp.logical_and(has_right, z >= zo)
        owner = z == zo
        both_sides = jnp.logical_and(from_left, from_right)
        one_left = jnp.logical_and(from_left, jnp.logical_not(from_right))
        one_right = jnp.logical_and(from_right, jnp.logical_not(from_left))
        neither = jnp.logical_not(jnp.logical_or(from_left, from_right))

        def reduce_piece(sub, carry):
            rightward, leftward = down_copies(k, sub)
            part_copy(k, sub).wait_recv()
            pl.when(from_left)(rightward.wait_recv)
            pl.when(from_right)(leftward.wait_recv)
            base = [piece(psend, b, sub), piece(ppart, seat(k), sub)]
            above = piece(pleft, seat(k), sub)
            below = piece(pright, seat(k), sub)

            def add(sources):
                value = sources[0][...].astype(F32)
                for source in sources[1:]:
                    value += source[...].astype(F32)
                return value.astype(BF16)

            def keep(sources):
                @pl.when(owner)
                def _():
                    piece(gp, b, sub)[...] = add(sources)

                @pl.when(jnp.logical_not(owner))
                def _():
                    piece(psum, seat(k), sub)[...] = add(sources)

            pl.when(neither)(lambda: keep(base))
            pl.when(one_left)(lambda: keep(base + [above]))
            pl.when(one_right)(lambda: keep(base + [below]))
            pl.when(both_sides)(lambda: keep(base + [above, below]))

            @pl.when(owner)
            def _():
                to_right, to_left, across = gp_copies(b, sub)
                pl.when(has_right)(to_right.start)
                pl.when(has_left)(to_left.start)
                across.start()

            pl.when(z < zo)(rightward.start)
            pl.when(z > zo)(leftward.start)
            return carry

        lax.fori_loop(0, subs, reduce_piece, 0)

    def spread(k):
        zo, co, b = place(k)

        def spread_piece(sub, carry):
            to_right, to_left, across = gp_copies(b, sub)
            across.wait_recv()
            pl.when(jnp.logical_and(z > zo, has_right))(to_right.start)
            pl.when(jnp.logical_and(z < zo, has_left))(to_left.start)
            across.start()
            return carry

        lax.fori_loop(0, subs, spread_piece, 0)

    def backward(k):
        zo, co, b = place(k)

        @pl.when(co != c)
        def _():
            for sub in range(subs):
                gp_copies(b, sub)[2].wait_recv()

        grad_low = jnp.zeros((hc, L), F32)
        for cols in col_chunks:
            gate = mod_row(2, 0, b, cols)
            low = gp[b, :, cols]
            weight = wo_s[:, cols].astype(F32)
            grad_low += dot_nt((weight * gate).astype(BF16), low)
            outer = dot_nn(ms[b], low)
            acc[3 * hc :, cols] += outer * gate
            gm[pl.ds(2 * B + b, 1), cols] = jnp.sum(weight * outer, axis=0, keepdims=True)
        grads = []
        for h in range(heads):
            queries, keys, values = [qs[b, h * 3 + j] for j in range(3)]
            exponent = et[b, h]
            inverse = rinv[b, h]
            rows = grad_low[h * HD : (h + 1) * HD].astype(BF16)
            probs_grad = dot_tn(values, rows)
            wide = exponent.astype(F32)
            delta = jnp.sum(wide * probs_grad, axis=0, keepdims=True) * inverse
            score_grad = (
                wide * (probs_grad - delta) * (inverse * (1.0 / math.sqrt(HD)))
            ).astype(BF16)
            grads.append(dot_nn(keys, score_grad))
            grads.append(dot_nt(queries, score_grad))
            grads.append(dot_nt((rows.astype(F32) * inverse).astype(BF16), exponent))
        act_grad = jnp.concatenate(grads, axis=0).astype(BF16)
        over_tokens = jnp.sum(act_grad.astype(F32), axis=1, keepdims=True)
        for cols in col_chunks:
            product = dot_nt(act_grad, nt[b, cols, :])
            weight = wq_s[:, cols].astype(F32)
            gm[pl.ds(b, 1), cols] = jnp.sum(weight * over_tokens, axis=0, keepdims=True)
            gm[pl.ds(B + b, 1), cols] = jnp.sum(weight * product, axis=0, keepdims=True)
            acc[: 3 * hc, cols] += product * (1.0 + mod_row(1, 0, b, cols)) + over_tokens * mod_row(
                0, 0, b, cols
            )

    def valid(k):
        return jnp.logical_and(k >= 0, k < B)

    def step(s, carry):
        @pl.when(s + 3 <= B)
        def _():
            send_own(s + 3, s + 3)

        for hop in range(1, nz):
            both(s - hop + 1, lambda which, sem, hop=hop: relay(which, sem, hop))

        def chain(i, inner):
            p = reach - i
            k = s - first_sum - CHAIN_GAP * p
            zo, co, b = place(k)
            mine = jnp.logical_and(co == c, chain_place(zo) == p)

            @pl.when(jnp.logical_and(valid(k), mine))
            def _():
                reduce_chain(k)

            return inner

        lax.fori_loop(0, reach + 1, chain, 0)

        def spreads(i, inner):
            away = reach - i
            k = s - first_spread - away
            zo, co, b = place(k)
            mine = jnp.logical_and(co == c, jnp.abs(z - zo) == away)

            @pl.when(jnp.logical_and(valid(k), mine))
            def _():
                spread(k)

            return inner

        lax.fori_loop(0, reach, spreads, 0)

        @pl.when(s == first_fwd)
        def _():
            wait_partner(None, 0)
            mr[...] = jnp.concatenate([mg[t] for t in range(n)], axis=0).T

        @pl.when(valid(s - first_fwd))
        def _():
            forward(s - first_fwd)

        @pl.when(valid(s - first_bwd))
        def _():
            backward(s - first_bwd)

        return carry

    lax.fori_loop(0, B + first_bwd, step, 0)

    mod_copies = []
    for t in range(n):
        mt_send[t] = gm[:, t * wp : (t + 1) * wp]
    for hop in range(1, n):
        peer = lax.rem(me + hop, n)
        mod_copies.append(
            remote(
                mt_send.at[peer],
                mt_land.at[hop - 1],
                mt_ssem.at[hop - 1],
                mt_rsem.at[hop - 1],
                peer,
            )
        )
        mod_copies[-1].start()

    for cols in col_chunks:
        grad_send[cols, :] = acc[:, cols].T.astype(BF16)
    grad_copies = []
    for hop in range(1, groups):
        peer = lax.rem(me_dp + hop, groups)
        start = peer * depth
        if depth % 16 == 0:
            start = pl.multiple_of(start, 16)
        grad_copies.append(
            remote_dp(
                grad_send.at[pl.ds(start, depth)],
                grad_land.at[hop - 1],
                dp_ssem.at[1, hop - 1],
                dp_rsem.at[1, hop - 1],
                peer,
            )
        )
        grad_copies[-1].start()

    for copy in mod_copies:
        copy.wait_recv()
    own_mod = mt_send[me]
    for hop in range(1, n):
        own_mod += mt_land[hop - 1]
    mod_land[me_dp] = own_mod
    wide_copies = []
    for hop in range(1, groups):
        peer = lax.rem(me_dp + hop, groups)
        wide_copies.append(
            remote_dp(
                mod_land.at[me_dp],
                mod_land.at[me_dp],
                dp_ssem.at[2, hop - 1],
                dp_rsem.at[2, hop - 1],
                peer,
            )
        )
        wide_copies[-1].start()

    def drain(ch, carry):
        both(ch, lambda which, sem: wait_own(which, sem))
        for hop in range(1, nz):
            both(ch, lambda which, sem, hop=hop: wait_relay(which, sem, hop))
        return carry

    lax.fori_loop(0, B + 1, drain, 0)

    def drain_sums(k, carry):
        zo, co, b = place(k)

        @pl.when(co != c)
        def _():
            for sub in range(subs):
                part_copy(k, sub).wait_send()

        @pl.when(co == c)
        def _():
            def drain_piece(sub, inner):
                pl.when(z != zo)(down_copies(k, sub)[0].wait_send)
                right_copy, left_copy, across = gp_copies(b, sub)
                pl.when(jnp.logical_and(z >= zo, has_right))(right_copy.wait_send)
                pl.when(jnp.logical_and(z <= zo, has_left))(left_copy.wait_send)
                across.wait_send()
                return inner

            lax.fori_loop(0, subs, drain_piece, 0)

        return carry

    lax.fori_loop(0, B, drain_sums, 0)
    for copy in mod_copies:
        copy.wait_send()
    for copy in act_copies + wide_copies:
        copy.wait()
    acts = jnp.concatenate([act_land[g].astype(F32) for g in range(groups)], axis=0)
    for kind in range(3):
        wide = jnp.concatenate(
            [mod_land[g, kind * B : (kind + 1) * B] for g in range(groups)], axis=0
        )
        out_ada[kind] = lax.dot_general(
            wide,
            acts,
            (((0,), (0,)), ((), ())),
            preferred_element_type=F32,
            precision=lax.Precision.HIGHEST,
        )
    start = me_dp * depth
    if depth % 16 == 0:
        start = pl.multiple_of(start, 16)
    total = grad_send[pl.ds(start, depth), :].astype(F32)
    for hop in range(1, groups):
        grad_copies[hop - 1].wait()
        total += grad_land[hop - 1].astype(F32)
    out_qkv[...] = total[:, : 3 * hc]
    out_go[...] = total[:, 3 * hc :].T


def round_up(value, unit):
    return (value + unit - 1) // unit * unit


def run_step(picks, noisy_t, guide_table, tables, ada, wq, wo):
    n = lax.axis_size("tensor")
    groups = lax.axis_size("dp")
    B, wp, L = noisy_t.shape
    D = wp * n
    hc = wo[0].shape[0]
    heads = hc // HD
    nz = n // 2
    seats = B // 2
    depth = D // groups
    assert B % 4 == 0 and n % 4 == 0
    lanes = round_up(9 * B, 128)
    scale_norm = 1.0 / math.sqrt(B * groups * L)
    sizes = (B, L, D, n, groups, heads, scale_norm)
    streamed = (*tables, *ada, *wq, *wo)
    dma = pltpu.SemaphoreType.DMA
    vmem = pltpu.VMEM
    scratch = [vmem(array.shape, array.dtype) for array in streamed] + [
        vmem((B, 128), F32),
        vmem((B, D), BF16),
        vmem((2 * B, D), BF16),
        vmem((groups, B, depth), BF16),
        vmem((groups, B, depth), BF16),
        vmem((groups, 3 * B, wp), F32),
        vmem((B, n, wp, L), BF16),
        vmem((n, wp, lanes), F32),
        vmem((lanes, D), F32),
        vmem((D, 8), F32),
        vmem((B, D, L), BF16),
        vmem((3, D, L), BF16),
        vmem((B, heads * 3, HD, L), BF16),
        vmem((B, heads, L, L), BF16),
        vmem((B, heads, 1, L), F32),
        vmem((B, hc, L), BF16),
        vmem((3 * hc, L), BF16),
        vmem((B, L, D), BF16),
        vmem((seats, L, D), BF16),
        vmem((seats, L, D), BF16),
        vmem((seats, L, D), BF16),
        vmem((seats, L, D), BF16),
        vmem((B, L, D), BF16),
        vmem((4 * hc, D), F32),
        vmem((3 * B, D), F32),
        vmem((n, 3 * B, wp), F32),
        vmem((n - 1, 3 * B, wp), F32),
        vmem((D, 4 * hc), BF16),
        vmem((groups - 1, depth, 4 * hc), BF16),
        dma((B + 1, 3 + 4 * (nz - 1))),
        dma((B + 1, n)),
        dma((seats, SUBS)),
        dma((seats, SUBS)),
        dma((seats, SUBS)),
        dma((seats, SUBS)),
        dma((seats, SUBS)),
        dma((B, SUBS, 3)),
        dma((B, SUBS)),
        dma((n - 1,)),
        dma((n - 1,)),
        dma((3, groups - 1)),
        dma((3, groups - 1)),
        dma((1,)),
        dma((len(streamed),)),
    ]
    return pl.pallas_call(
        functools.partial(step_kernel, sizes),
        out_shape=[
            jax.ShapeDtypeStruct((depth, 3 * hc), F32),
            jax.ShapeDtypeStruct((hc, depth), F32),
            jax.ShapeDtypeStruct((3, wp, depth), F32),
        ],
        in_specs=[pl.BlockSpec(memory_space=pltpu.VMEM)] * (len(picks) + 2)
        + [pl.BlockSpec(memory_space=pl.ANY)] * len(streamed),
        out_specs=[pl.BlockSpec(memory_space=pltpu.VMEM)] * 3,
        scratch_shapes=scratch,
        compiler_params=pltpu.CompilerParams(
            collective_id=0, has_side_effects=True, vmem_limit_bytes=62 * 1024 * 1024
        ),
    )(*picks, noisy_t, guide_table, *streamed)


def local(
    noisy,
    labels,
    tsteps,
    guide_index,
    class_table,
    time_table,
    guide_table,
    guide_weights,
    teacher_qkv,
    teacher_out,
    teacher_ada,
    student_qkv,
    student_out,
    student_ada,
):
    grad_qkv, grad_out, grad_ada = run_step(
        (labels[:, None], tsteps[:, None], guide_index[:, None], guide_weights[None, :]),
        noisy.transpose(0, 2, 1),
        guide_table,
        (class_table, time_table),
        (student_ada.transpose(0, 2, 1), teacher_ada.transpose(0, 2, 1)),
        (student_qkv.T, teacher_qkv.T),
        (student_out, teacher_out),
    )
    return grad_qkv, grad_out, grad_ada.transpose(0, 2, 1)


def solution(mesh):
    return jax.shard_map(
        local,
        mesh=mesh,
        in_specs=(
            P("dp", None, "tensor"),
            P("dp"),
            P("dp"),
            P("dp"),
            P(),
            P(),
            P(),
            P(),
            P(None, "tensor"),
            P("tensor", None),
            P(None, None, "tensor"),
            P(None, "tensor"),
            P("tensor", None),
            P(None, None, "tensor"),
        ),
        out_specs=(P("dp", "tensor"), P("tensor", "dp"), P(None, "dp", "tensor")),
        check_vma=False,
    )
```

time: 187 us -> 158 us (0.84)
  Pallas kernels: 171 us -> 148 us
  matrix products: 5.61 us -> 0 us
    pallas_call x1, Pallas kernels: 171 us -> 148 us  [run_step(): pl.pallas_call(functools.partial(step_kernel, sizes), out_shape=[jax.Shap...]
    dot_general x4 -> x0, matrix products: 5.61 us -> none  [the longest x2 2.68 us: lookup_rows(): return jnp.dot(one_hot, table_rows, preferred_element_type=F32)]
    broadcast_in_dim x1 -> x3, local copies, waits for them, and re-layouts: 0.67 us -> 3.96 us  [the longest x1 1.32 us: local(): labels[:, None]]
    unnamed x20 -> x3, local copies, waits for them, and re-layouts: 6.1 us -> 5.52 us
where the time goes in v2:
time: 158 us
  Pallas kernels  148 us (94%)
  local copies, waits for them, and re-layouts  9.49 us (6%)
    pallas_call x1, Pallas kernels, run_step(): pl.pallas_call(functools.partial(step_kernel, sizes), out_shape=[jax.Shap...  148 us
    unnamed x3, local copies, waits for them, and re-layouts  5.52 us

profile of v2, /device:TPU:0, one launch (start us, length us, event | category | flops | bytes accessed | tf_op | source)
XLA Modules:
  0.0 158.0 jit_solution(13900343150187431413)
XLA Ops:
  0.6 1.3 copy.17.labels
  2.0 1.3 copy.18.tsteps
  3.3 1.3 copy.19.guide_index
  4.6 147.9 %shard_map.157 = (f32[288,432]{1,0:T(8,128)}, f32[144,288]{1,0:T(8,128)}, f32[3,144,288]{2,1,0:T(8,128)}) custom-call(s32[8,1]{1,0:T(8,128)} %copy.17.labels, s32[8,1]{1,0:T(8,128)} %copy.18.tsteps, s32[8,1]{1,0:T(8,128)} %copy.19.guide_index, f32[1,32]{1,0:T(1,128)} %bitcast.16, bf16[8,144,256]{2,1,0:T(8,128)(2,1)} %bitcast.15, ...), custom_call_target="tpu_custom_call" | custom-call | tf_op jit(solution)/shard_map/pallas_call | solution.py:774
  152.5 1.9 %copy.23 = f32[288,432]{1,0:T(8,128)} copy(f32[288,432]{1,0:T(8,128)} %get-tuple-element.12) | data formatting | bytes 995328
  154.4 1.6 %copy.24 = f32[144,288]{1,0:T(8,128)} copy(f32[144,288]{1,0:T(8,128)} %get-tuple-element.13) | data formatting | bytes 331776
  156.1 2.0 %copy.25 = f32[3,288,144]{1,2,0:T(8,128)} copy(f32[3,288,144]{1,2,0:T(8,128)} %bitcast.14) | data formatting | bytes 995328

commit v3 on v2

--- a/solution.py
+++ b/solution.py
@@ -47,9 +47,9 @@
     wq_t_hbm,
     wo_s_hbm,
     wo_t_hbm,
-    out_qkv,
-    out_go,
-    out_ada,
+    grad_land,
+    act_land,
+    mod_land,
     class_table,
     time_table,
     ada_s,
@@ -62,8 +62,6 @@
     act_s,
     act_t,
     act_send,
-    act_land,
-    mod_land,
     xt,
     mg,
     mr,
@@ -86,7 +84,6 @@
     mt_send,
     mt_land,
     grad_send,
-    grad_land,
     ag_send,
     ag_recv,
     pt_send,
@@ -274,24 +271,33 @@
     def silu(value):
         return value / (1.0 + jnp.exp(-value))
 
+    diagonal = lax.broadcasted_iota(jnp.int32, (B, B), 0) == lax.broadcasted_iota(
+        jnp.int32, (B, B), 1
+    )
+
+    def as_column(row):
+        wide = jnp.broadcast_to(row[...].astype(F32), (B, B))
+        return jnp.sum(jnp.where(diagonal, wide, 0.0), axis=1, keepdims=True).astype(jnp.int32)
+
     def lookup(table, indices):
         count = table.shape[0]
         even = count // 16 * 16
         spots = lax.broadcasted_iota(jnp.int32, (B, even), 1)
-        found = dot_nn((spots == indices[...]).astype(F32).astype(BF16), table[:even, :])
+        found = dot_nn((spots == indices).astype(F32).astype(BF16), table[:even, :])
         for row in range(even, count):
-            found += jnp.where(indices[...] == row, table[row : row + 1, :].astype(F32), 0.0)
+            found += jnp.where(indices == row, table[row : row + 1, :].astype(F32), 0.0)
         return found
 
     last = class_table.shape[0] - 1
-    time_embed = lookup(time_table, tsteps)
-    cond_embed = lookup(class_table, labels) + time_embed
+    time_embed = lookup(time_table, as_column(tsteps))
+    cond_embed = lookup(class_table, as_column(labels)) + time_embed
     null_embed = class_table[last : last + 1, :].astype(F32) + time_embed
-    student_embed = cond_embed + lookup(guide_table, guide_index)
+    guide_column = as_column(guide_index)
+    student_embed = cond_embed + lookup(guide_table, guide_column)
     act_s[...] = silu(student_embed).astype(BF16)
     act_t[...] = silu(jnp.concatenate([cond_embed, null_embed], axis=0)).astype(BF16)
     guides = guide_weights.shape[1]
-    guide_spots = lax.broadcasted_iota(jnp.int32, (B, guides), 1) == guide_index[...]
+    guide_spots = lax.broadcasted_iota(jnp.int32, (B, guides), 1) == guide_column
     strength[...] = jnp.broadcast_to(
         jnp.sum(jnp.where(guide_spots, guide_weights[...], 0.0), axis=1, keepdims=True), (B, 128)
     )
@@ -299,8 +305,8 @@
         load.wait()
     for kind in range(3):
         start = kind * 3 * B
-        mg[me, :, start : start + B] = dot_nt(ada_s[kind], act_s[...])
-        mg[me, :, start + B : start + 3 * B] = dot_nt(ada_t[kind], act_t[...])
+        mg[me, :, start : start + B] = dot_nt(ada_s[kind], act_s[...]).astype(BF16)
+        mg[me, :, start + B : start + 3 * B] = dot_nt(ada_t[kind], act_t[...]).astype(BF16)
     send_own(None, 0)
     for g in range(groups):
         act_send[g] = act_s[:, g * depth : (g + 1) * depth]
@@ -543,7 +549,7 @@
         def _():
             send_own(s + 3, s + 3)
 
-        for hop in range(1, nz):
+        for hop in range(nz - 1, 0, -1):
             both(s - hop + 1, lambda which, sem, hop=hop: relay(which, sem, hop))
 
         def chain(i, inner):
@@ -577,7 +583,7 @@
         @pl.when(s == first_fwd)
         def _():
             wait_partner(None, 0)
-            mr[...] = jnp.concatenate([mg[t] for t in range(n)], axis=0).T
+            mr[...] = jnp.concatenate([mg[t].astype(F32) for t in range(n)], axis=0).T
 
         @pl.when(valid(s - first_fwd))
         def _():
@@ -618,7 +624,7 @@
         grad_copies.append(
             remote_dp(
                 grad_send.at[pl.ds(start, depth)],
-                grad_land.at[hop - 1],
+                grad_land.at[me_dp],
                 dp_ssem.at[1, hop - 1],
                 dp_rsem.at[1, hop - 1],
                 peer,
@@ -681,6 +687,22 @@
         copy.wait_send()
     for copy in act_copies + wide_copies:
         copy.wait()
+    start = me_dp * depth
+    if depth % 16 == 0:
+        start = pl.multiple_of(start, 16)
+    grad_land[me_dp] = grad_send[pl.ds(start, depth), :]
+    for copy in grad_copies:
+        copy.wait()
+
+
+def finish_kernel(grad_land, act_land, mod_land, out_qkv, out_go, out_ada):
+    groups, B, _ = act_land.shape
+    total = grad_land[0].astype(F32)
+    for g in range(1, groups):
+        total += grad_land[g].astype(F32)
+    width = out_qkv.shape[1]
+    out_qkv[...] = total[:, :width]
+    out_go[...] = total[:, width:].T
     acts = jnp.concatenate([act_land[g].astype(F32) for g in range(groups)], axis=0)
     for kind in range(3):
         wide = jnp.concatenate(
@@ -693,15 +715,6 @@
             preferred_element_type=F32,
             precision=lax.Precision.HIGHEST,
         )
-    start = me_dp * depth
-    if depth % 16 == 0:
-        start = pl.multiple_of(start, 16)
-    total = grad_send[pl.ds(start, depth), :].astype(F32)
-    for hop in range(1, groups):
-        grad_copies[hop - 1].wait()
-        total += grad_land[hop - 1].astype(F32)
-    out_qkv[...] = total[:, : 3 * hc]
-    out_go[...] = total[:, 3 * hc :].T
 
 
 def round_up(value, unit):
@@ -730,10 +743,8 @@
         vmem((B, D), BF16),
         vmem((2 * B, D), BF16),
         vmem((groups, B, depth), BF16),
-        vmem((groups, B, depth), BF16),
-        vmem((groups, 3 * B, wp), F32),
         vmem((B, n, wp, L), BF16),
-        vmem((n, wp, lanes), F32),
+        vmem((n, wp, lanes), BF16),
         vmem((lanes, D), F32),
         vmem((D, 8), F32),
         vmem((B, D, L), BF16),
@@ -754,7 +765,6 @@
         vmem((n, 3 * B, wp), F32),
         vmem((n - 1, 3 * B, wp), F32),
         vmem((D, 4 * hc), BF16),
-        vmem((groups - 1, depth, 4 * hc), BF16),
         dma((B + 1, 3 + 4 * (nz - 1))),
         dma((B + 1, n)),
         dma((seats, SUBS)),
@@ -771,21 +781,32 @@
         dma((1,)),
         dma((len(streamed),)),
     ]
+    vmem_spec = pl.BlockSpec(memory_space=pltpu.VMEM)
+    landed = pl.pallas_call(
+        functools.partial(step_kernel, sizes),
+        out_shape=[
+            jax.ShapeDtypeStruct((groups, depth, 4 * hc), BF16),
+            jax.ShapeDtypeStruct((groups, B, depth), BF16),
+            jax.ShapeDtypeStruct((groups, 3 * B, wp), F32),
+        ],
+        in_specs=[vmem_spec] * (len(picks) + 2)
+        + [pl.BlockSpec(memory_space=pl.ANY)] * len(streamed),
+        out_specs=[vmem_spec] * 3,
+        scratch_shapes=scratch,
+        compiler_params=pltpu.CompilerParams(
+            collective_id=0, has_side_effects=True, vmem_limit_bytes=62 * 1024 * 1024
+        ),
+    )(*picks, noisy_t, guide_table, *streamed)
     return pl.pallas_call(
-        functools.partial(step_kernel, sizes),
+        finish_kernel,
         out_shape=[
             jax.ShapeDtypeStruct((depth, 3 * hc), F32),
             jax.ShapeDtypeStruct((hc, depth), F32),
             jax.ShapeDtypeStruct((3, wp, depth), F32),
         ],
-        in_specs=[pl.BlockSpec(memory_space=pltpu.VMEM)] * (len(picks) + 2)
-        + [pl.BlockSpec(memory_space=pl.ANY)] * len(streamed),
-        out_specs=[pl.BlockSpec(memory_space=pltpu.VMEM)] * 3,
-        scratch_shapes=scratch,
-        compiler_params=pltpu.CompilerParams(
-            collective_id=0, has_side_effects=True, vmem_limit_bytes=62 * 1024 * 1024
-        ),
-    )(*picks, noisy_t, guide_table, *streamed)
+        in_specs=[vmem_spec] * 3,
+        out_specs=[vmem_spec] * 3,
+    )(*landed)
 
 
 def local(
@@ -805,7 +826,7 @@
     student_ada,
 ):
     grad_qkv, grad_out, grad_ada = run_step(
-        (labels[:, None], tsteps[:, None], guide_index[:, None], guide_weights[None, :]),
+        (labels[None, :], tsteps[None, :], guide_index[None, :], guide_weights[None, :]),
         noisy.transpose(0, 2, 1),
         guide_table,
         (class_table, time_table),

time: 158 us -> 149 us (0.943)
  local copies, waits for them, and re-layouts: 9.49 us -> 0 us
    unnamed x3 -> x0, local copies, waits for them, and re-layouts: 5.52 us -> none
    broadcast_in_dim x3 -> x0, local copies, waits for them, and re-layouts: 3.96 us -> none  [the longest x1 1.32 us: local(): labels[:, None]]
    pallas_call x0 -> x1, Pallas kernels: none -> 3.18 us  [run_step(): pl.pallas_call(finish_kernel, out_shape=[jax.ShapeDtypeStruct((depth, 3 *...]
    pallas_call x1, Pallas kernels: 148 us -> 145 us  [run_step(): pl.pallas_call(functools.partial(step_kernel, sizes), out_shape=[jax.Shap...]
where the time goes in v3:
time: 149 us
  Pallas kernels  148 us (99%)
    pallas_call x1, Pallas kernels, run_step(): pl.pallas_call(functools.partial(step_kernel, sizes), out_shape=[jax.Shap...  145 us
    pallas_call x1, Pallas kernels, run_step(): pl.pallas_call(finish_kernel, out_shape=[jax.ShapeDtypeStruct((depth, 3 *...  3.18 us

profile of v3, /device:TPU:0, one launch (start us, length us, event | category | flops | bytes accessed | tf_op | source)
XLA Modules:
  0.0 148.6 jit_solution(10117831789532840812)
XLA Ops:
  0.6 144.8 %shard_map.157 = (bf16[4,288,576]{2,1,0:T(8,128)(2,1)}, bf16[4,8,288]{2,1,0:T(8,128)(2,1)}, f32[4,24,144]{2,1,0:T(8,128)}) custom-call(s32[1,8]{1,0:T(1,128)} %bitcast.15, s32[1,8]{1,0:T(1,128)} %bitcast.16, s32[1,8]{1,0:T(1,128)} %bitcast.17, f32[1,32]{1,0:T(1,128)} %bitcast.18, bf16[8,144,256]{2,1,0:T(8,128)(2,1)} %bitcast.14, ...), custom_call_target="tpu_custom_call" | custom-call | tf_op jit(solution)/shard_map/pallas_call | solution.py:785
  145.4 3.2 %shard_map.158 = (f32[288,432]{1,0:T(8,128)}, f32[144,288]{1,0:T(8,128)}, f32[3,144,288]{2,1,0:T(8,128)}) custom-call(bf16[4,288,576]{2,1,0:T(8,128)(2,1)} %get-tuple-element.9.grad_land, bf16[4,8,288]{2,1,0:T(8,128)(2,1)} %get-tuple-element.10.act_land, f32[4,24,144]{2,1,0:T(8,128)} %get-tuple-element.11.mod_land), custom_call_target="tpu_custom_call" | custom-call | tf_op jit(solution)/shard_map/pallas_call | solution.py:800

commit v4 on v3

--- a/solution.py
+++ b/solution.py
@@ -17,6 +17,8 @@
 LOG2E = math.log2(math.e)
 SUBS = 2
 CHAIN_GAP = 2
+SPREAD_GAP = 2
+BACK_GAP = 0
 
 
 def dot_nn(a, b):
@@ -48,6 +50,7 @@
     wo_s_hbm,
     wo_t_hbm,
     grad_land,
+    rest_land,
     act_land,
     mod_land,
     class_table,
@@ -84,6 +87,8 @@
     mt_send,
     mt_land,
     grad_send,
+    rest_rows,
+    rest_send,
     ag_send,
     ag_recv,
     pt_send,
@@ -120,7 +125,7 @@
     first_sum = nz + 1
     reach = nz // 2
     first_spread = first_sum + CHAIN_GAP * reach
-    first_bwd = first_spread + reach + 1
+    first_bwd = first_spread + 1 + SPREAD_GAP * (reach - 1) + BACK_GAP
     soft = LOG2E / math.sqrt(HD)
     subs = SUBS
     row_step = L // subs
@@ -168,7 +173,7 @@
             ]
         )
     ]
-    for load in loads:
+    for load in loads[:4]:
         load.start()
     barrier = pltpu.get_barrier_semaphore()
     for hop in range(1, n):
@@ -263,10 +268,11 @@
         send_own(jnp.int32(ch), ch)
     own_rows = pltpu.make_async_copy(noisy, xt.at[:, me], own_sem.at[0])
     own_rows.start()
-    acc[...] = jnp.zeros_like(acc)
     mg[me] = jnp.zeros_like(mg[me])
     for load in loads[:2]:
         load.wait()
+    for load in loads[4:]:
+        load.start()
 
     def silu(value):
         return value / (1.0 + jnp.exp(-value))
@@ -301,13 +307,14 @@
     strength[...] = jnp.broadcast_to(
         jnp.sum(jnp.where(guide_spots, guide_weights[...], 0.0), axis=1, keepdims=True), (B, 128)
     )
-    for load in loads[2:]:
+    for load in loads[2:4]:
         load.wait()
     for kind in range(3):
         start = kind * 3 * B
         mg[me, :, start : start + B] = dot_nt(ada_s[kind], act_s[...]).astype(BF16)
         mg[me, :, start + B : start + 3 * B] = dot_nt(ada_t[kind], act_t[...]).astype(BF16)
     send_own(None, 0)
+    acc[...] = jnp.zeros_like(acc)
     for g in range(groups):
         act_send[g] = act_s[:, g * depth : (g + 1) * depth]
     act_copies = []
@@ -325,6 +332,8 @@
         act_copies[-1].start()
     act_land[me_dp] = act_send[me_dp]
     own_rows.wait()
+    for load in loads[4:]:
+        load.wait()
 
     def mod_row(kind, model, b, cols):
         return mr[pl.ds((kind * 3 + model) * B + b, 1), cols]
@@ -568,7 +577,7 @@
 
         def spreads(i, inner):
             away = reach - i
-            k = s - first_spread - away
+            k = s - first_spread - 1 - SPREAD_GAP * (away - 1)
             zo, co, b = place(k)
             mine = jnp.logical_and(co == c, jnp.abs(z - zo) == away)
 
@@ -613,24 +622,47 @@
         )
         mod_copies[-1].start()
 
+    def grad_copy(g):
+        return remote_dp(
+            grad_send.at[pl.ds(g * depth, depth)],
+            grad_land.at[me_dp],
+            dp_ssem.at[1, g],
+            dp_rsem.at[1, me_dp],
+            g,
+        )
+
+    def rest_copy(g):
+        return remote_dp(
+            rest_send.at[g], rest_land.at[me_dp], dp_ssem.at[3, g], dp_rsem.at[3, me_dp], g
+        )
+
+    def arrivals(g):
+        block, rest = grad_land.at[g], rest_land.at[g]
+        return (
+            remote_dp(block, block, dp_ssem.at[1, g], dp_rsem.at[1, g], g),
+            remote_dp(rest, rest, dp_ssem.at[3, g], dp_rsem.at[3, g], g),
+        )
+
+    main = grad_send.shape[1]
+    half = depth // 2
+
+    sent = 0
     for cols in col_chunks:
-        grad_send[cols, :] = acc[:, cols].T.astype(BF16)
-    grad_copies = []
-    for hop in range(1, groups):
-        peer = lax.rem(me_dp + hop, groups)
-        start = peer * depth
-        if depth % 16 == 0:
-            start = pl.multiple_of(start, 16)
-        grad_copies.append(
-            remote_dp(
-                grad_send.at[pl.ds(start, depth)],
-                grad_land.at[me_dp],
-                dp_ssem.at[1, hop - 1],
-                dp_rsem.at[1, hop - 1],
-                peer,
-            )
-        )
-        grad_copies[-1].start()
+        turned = acc[:, cols].T
+        grad_send[cols, :] = turned[:, :main].astype(BF16)
+        rest_rows[cols, :] = turned[:, turned.shape[1] - 64 :]
+        while sent < groups and (sent + 1) * depth <= cols.start + cols.size:
+            first, middle = sent * depth, sent * depth + half
+            rest_send[sent] = jnp.concatenate(
+                [rest_rows[first:middle, :], rest_rows[middle : middle + half, :]], axis=1
+            ).astype(BF16)
+
+            @pl.when(me_dp != sent)
+            def _(g=sent):
+                grad_copy(g).start()
+                rest_copy(g).start()
+
+            sent += 1
 
     for copy in mod_copies:
         copy.wait_recv()
@@ -691,18 +723,32 @@
     if depth % 16 == 0:
         start = pl.multiple_of(start, 16)
     grad_land[me_dp] = grad_send[pl.ds(start, depth), :]
-    for copy in grad_copies:
-        copy.wait()
-
-
-def finish_kernel(grad_land, act_land, mod_land, out_qkv, out_go, out_ada):
+    rest_land[me_dp] = rest_send[me_dp]
+    for g in range(groups):
+
+        @pl.when(me_dp != g)
+        def _(g=g):
+            grad_copy(g).wait_send()
+            rest_copy(g).wait_send()
+            for arrival in arrivals(g):
+                arrival.wait_recv()
+
+
+def finish_kernel(grad_land, rest_land, act_land, mod_land, out_qkv, out_go, out_ada):
     groups, B, _ = act_land.shape
     total = grad_land[0].astype(F32)
     for g in range(1, groups):
         total += grad_land[g].astype(F32)
     width = out_qkv.shape[1]
     out_qkv[...] = total[:, :width]
-    out_go[...] = total[:, width:].T
+    if total.shape[1] == width + out_go.shape[0]:
+        out_go[...] = total[:, width:].T
+    else:
+        rest = rest_land[0].astype(F32)
+        for g in range(1, groups):
+            rest += rest_land[g].astype(F32)
+        rest = jnp.concatenate([rest[:, :64], rest[:, 64:]], axis=0)
+        out_go[...] = jnp.concatenate([total[:, width:].T, rest.T], axis=0)
     acts = jnp.concatenate([act_land[g].astype(F32) for g in range(groups)], axis=0)
     for kind in range(3):
         wide = jnp.concatenate(
@@ -730,6 +776,7 @@
     heads = hc // HD
     nz = n // 2
     seats = B // 2
+    main = 4 * hc - 64 if 4 * hc % 128 == 64 else 4 * hc
     depth = D // groups
     assert B % 4 == 0 and n % 4 == 0
     lanes = round_up(9 * B, 128)
@@ -764,7 +811,9 @@
         vmem((3 * B, D), F32),
         vmem((n, 3 * B, wp), F32),
         vmem((n - 1, 3 * B, wp), F32),
-        vmem((D, 4 * hc), BF16),
+        vmem((D, main), BF16),
+        vmem((D, 64), F32),
+        vmem((groups, depth // 2, 128), BF16),
         dma((B + 1, 3 + 4 * (nz - 1))),
         dma((B + 1, n)),
         dma((seats, SUBS)),
@@ -776,8 +825,8 @@
         dma((B, SUBS)),
         dma((n - 1,)),
         dma((n - 1,)),
-        dma((3, groups - 1)),
-        dma((3, groups - 1)),
+        dma((4, groups)),
+        dma((4, groups)),
         dma((1,)),
         dma((len(streamed),)),
     ]
@@ -785,13 +834,14 @@
     landed = pl.pallas_call(
         functools.partial(step_kernel, sizes),
         out_shape=[
-            jax.ShapeDtypeStruct((groups, depth, 4 * hc), BF16),
+            jax.ShapeDtypeStruct((groups, depth, main), BF16),
+            jax.ShapeDtypeStruct((groups, depth // 2, 128), BF16),
             jax.ShapeDtypeStruct((groups, B, depth), BF16),
             jax.ShapeDtypeStruct((groups, 3 * B, wp), F32),
         ],
         in_specs=[vmem_spec] * (len(picks) + 2)
         + [pl.BlockSpec(memory_space=pl.ANY)] * len(streamed),
-        out_specs=[vmem_spec] * 3,
+        out_specs=[vmem_spec] * 4,
         scratch_shapes=scratch,
         compiler_params=pltpu.CompilerParams(
             collective_id=0, has_side_effects=True, vmem_limit_bytes=62 * 1024 * 1024
@@ -804,7 +854,7 @@
             jax.ShapeDtypeStruct((hc, depth), F32),
             jax.ShapeDtypeStruct((3, wp, depth), F32),
         ],
-        in_specs=[vmem_spec] * 3,
+        in_specs=[vmem_spec] * 4,
         out_specs=[vmem_spec] * 3,
     )(*landed)
 

time: 149 us -> 147 us (0.987)
  Pallas kernels: 148 us -> 146 us
    pallas_call x1, Pallas kernels: 145 us -> 143 us  [run_step(): pl.pallas_call(functools.partial(step_kernel, sizes), out_shape=[jax.Shap...]
where the time goes in v4:
time: 147 us
  Pallas kernels  146 us (99%)
    pallas_call x1, Pallas kernels, run_step(): pl.pallas_call(functools.partial(step_kernel, sizes), out_shape=[jax.Shap...  143 us
    pallas_call x1, Pallas kernels, run_step(): pl.pallas_call(finish_kernel, out_shape=[jax.ShapeDtypeStruct((depth, 3 *...  3.15 us

profile of v4, /device:TPU:0, one launch (start us, length us, event | category | flops | bytes accessed | tf_op | source)
XLA Modules:
  0.0 147.1 jit_solution(14691450173701725779)
XLA Ops:
  0.6 143.3 %shard_map.157 = (bf16[4,288,512]{2,1,0:T(8,128)(2,1)}, bf16[4,144,128]{2,1,0:T(8,128)(2,1)}, bf16[4,8,288]{2,1,0:T(8,128)(2,1)}, f32[4,24,144]{2,1,0:T(8,128)}) custom-call(s32[1,8]{1,0:T(1,128)} %bitcast.15, s32[1,8]{1,0:T(1,128)} %bitcast.16, s32[1,8]{1,0:T(1,128)} %bitcast.17, f32[1,32]{1,0:T(1,128)} %bitcast.18, bf16[8,144,256]{2,1,0:T(8,128)(2,1)} %bitcast.14, ...), custom_call_target="tpu_custom_call" | custom-call | tf_op jit(solution)/shard_map/pallas_call | solution.py:834
  143.9 3.2 %shard_map.158 = (f32[288,432]{1,0:T(8,128)}, f32[144,288]{1,0:T(8,128)}, f32[3,144,288]{2,1,0:T(8,128)}) custom-call(bf16[4,288,512]{2,1,0:T(8,128)(2,1)} %get-tuple-element.10.grad_land, bf16[4,144,128]{2,1,0:T(8,128)(2,1)} %get-tuple-element.11.rest_land, bf16[4,8,288]{2,1,0:T(8,128)(2,1)} %get-tuple-element.12.act_land, ...), custom_call_target="tpu_custom_call" | custom-call | tf_op jit(solution)/shard_map/pallas_call | solution.py:850
